TPU v7x, 32 devices: a whole 2x2x4 slice. The times are simulated.
32 devices in a mesh: vp: 4 (over z), dp: 8 (over y, x, core).
Axes of the slice: x: 2, y: 2, z: 4, core: 2. Of those that a mesh axis runs over, the one named last changes fastest.
Arguments:
- h_last: bfloat16 [4096, 49, 1024], P('dp')
- ln_gamma: float32 [1024], replicated
- ln_beta: float32 [1024], replicated
- w_cls: bfloat16 [1024, 22016], P(None, 'vp')
- b_cls: float32 [22016], P('vp')
- targets: float32 [4096, 22016], P('dp', 'vp')
Outputs:
- output 1: float32 [], replicated
- output 2: float32 [1024, 22016], P(None, 'vp')
- output 3: float32 [22016], P('vp')
- output 4: bfloat16 [4096, 49, 1024], P('dp')
All inputs are finite; a program needn't handle non-finite values.
Results may differ from a plain program's by a relative error of at most 0.001.
Values sent between devices are 32-bit elements.
A program may use at most 1 GiB of HBM per device.

v0:
```python
import functools

import jax
import jax.numpy as jnp
from jax import lax
from jax.experimental import pallas as pl
from jax.experimental.pallas import tpu as pltpu
from jax.sharding import PartitionSpec as P


NUM_CLASSES = 21841
LN_EPS = 1e-5
F32 = jnp.float32
BF16 = jnp.bfloat16
MESH = pl.DeviceIdType.MESH


def norm_rows(x):
    width = x.shape[-1]
    c = x - x.sum(axis=-1, keepdims=True) * (1.0 / width)
    var = (c * c).sum(axis=-1, keepdims=True) * (1.0 / width)
    return c, lax.rsqrt(var + LN_EPS)


def pool_kernel(h_ref, gamma_ref, beta_ref, u_ref, acc_ref):
    tokens, rows, _ = h_ref.shape
    acc_ref[...] = jnp.zeros_like(acc_ref)

    def group(i, carry):
        here = pl.ds(pl.multiple_of(i * 16, 16), 16)
        for t in range(tokens):
            c, r = norm_rows(h_ref[t, here, :].astype(F32))
            acc_ref[here, :] += c * r
        return carry

    lax.fori_loop(0, rows // 16, group, 0)
    u = acc_ref[...] * (gamma_ref[...] * (1.0 / tokens)) + beta_ref[...]
    u_ref[...] = u.astype(BF16)


def pool_forward(ht, gamma, beta, rows=32):
    tokens, images, width = ht.shape
    rows = min(rows, images)
    return pl.pallas_call(
        pool_kernel,
        grid=(images // rows,),
        in_specs=[
            pl.BlockSpec((tokens, rows, width), lambda i: (0, i, 0)),
            pl.BlockSpec((1, width), lambda i: (0, 0)),
            pl.BlockSpec((1, width), lambda i: (0, 0)),
        ],
        out_specs=pl.BlockSpec((rows, width), lambda i: (i, 0)),
        out_shape=jax.ShapeDtypeStruct((images, width), BF16),
        scratch_shapes=[pltpu.VMEM((rows, width), F32)],
        compiler_params=pltpu.CompilerParams(dimension_semantics=("arbitrary",)),
        cost_estimate=pl.CostEstimate(flops=8 * ht.size * 40, bytes_accessed=2 * ht.size, transcendentals=0),
        name="pool_forward",
    )(ht, gamma[None], beta[None])


def pool_backward_kernel(off_ref, h_ref, du_ref, gamma_ref, *rest):
    dh_ref, token_ref, v_ref = rest[-3:]
    tokens, rows, width = h_ref.shape
    v = du_ref[...] * (gamma_ref[...] * (1.0 / tokens))
    v_ref[...] = v - v.sum(axis=-1, keepdims=True) * (1.0 / width)
    token_ref[...] = jnp.zeros_like(token_ref)

    def group(i, carry):
        here = pl.ds(pl.multiple_of(i * 16, 16), 16)
        for t in range(tokens):
            c, r = norm_rows(h_ref[t, here, :].astype(F32))
            vc = v_ref[here, :]
            xhat = c * r
            k = (vc * xhat).sum(axis=-1, keepdims=True) * (1.0 / width)
            dh_ref[t, here, :] = ((vc - xhat * k) * r).astype(BF16)
        return carry

    lax.fori_loop(0, rows // 16, group, 0)


def pool_backward(ht, du, gamma, buf, block, after, rows=32):
    tokens, images, width = ht.shape
    count = du.shape[0]
    rows = min(rows, count)
    steps = count // rows
    any_spec = pl.BlockSpec(memory_space=pl.ANY)
    in_specs = [
        pl.BlockSpec((tokens, rows, width), lambda i, o: (0, o[0] + i, 0)),
        pl.BlockSpec((rows, width), lambda i, o: (i, 0)),
        pl.BlockSpec((1, width), lambda i, o: (0, 0)),
        any_spec,
    ]
    args = [(block * steps).astype(jnp.int32)[None], ht, du, gamma[None], after]
    aliases = {}
    if buf is not None:
        in_specs.append(any_spec)
        args.append(buf)
        aliases = {5: 0}
    return pl.pallas_call(
        pool_backward_kernel,
        grid_spec=pltpu.PrefetchScalarGridSpec(
            num_scalar_prefetch=1,
            grid=(steps,),
            in_specs=in_specs,
            out_specs=[
                pl.BlockSpec((tokens, rows, width), lambda i, o: (0, o[0] + i, 0)),
                pl.BlockSpec((8, 128), lambda i, o: (0, 0)),
            ],
            scratch_shapes=[pltpu.VMEM((rows, width), F32)],
        ),
        out_shape=[
            jax.ShapeDtypeStruct((tokens, images, width), BF16),
            jax.ShapeDtypeStruct((8, 128), F32),
        ],
        input_output_aliases=aliases,
        compiler_params=pltpu.CompilerParams(dimension_semantics=("arbitrary",)),
        cost_estimate=pl.CostEstimate(
            flops=40 * 12 * tokens * count * width, bytes_accessed=4 * tokens * count * width, transcendentals=0
        ),
        name="pool_backward",
    )(*args)


def add_kernel(a_ref, b_ref, c_ref, *rest):
    rest[-1][...] = (a_ref[...] + b_ref[...]) + c_ref[...]


def add_after(a, b, c, *after, rows=32):
    n = a.shape[1]
    spec = pl.BlockSpec((rows, n), lambda i: (i, 0))
    return pl.pallas_call(
        add_kernel,
        grid=(a.shape[0] // rows,),
        in_specs=[spec] * 3 + [pl.BlockSpec(memory_space=pl.ANY)] * len(after),
        out_specs=spec,
        out_shape=jax.ShapeDtypeStruct(a.shape, a.dtype),
        cost_estimate=pl.CostEstimate(flops=10 * a.size, bytes_accessed=16 * a.size, transcendentals=0),
        name="add_after",
    )(a, b, c, *after)


def place_kernel(off_ref, v_ref, o_ref):
    o_ref[...] = v_ref[...]


def place_first(v, block, total_rows, rows=32):
    count, n = v.shape
    steps = count // rows
    return pl.pallas_call(
        place_kernel,
        grid_spec=pltpu.PrefetchScalarGridSpec(
            num_scalar_prefetch=1,
            grid=(steps,),
            in_specs=[pl.BlockSpec((rows, n), lambda i, o: (i, 0))],
            out_specs=pl.BlockSpec((rows, n), lambda i, o: (o[0] + i, 0)),
        ),
        out_shape=jax.ShapeDtypeStruct((total_rows, n), v.dtype),
        cost_estimate=pl.CostEstimate(flops=10 * v.size, bytes_accessed=8 * v.size, transcendentals=0),
        name="place_first",
    )((block * steps).astype(jnp.int32)[None], v)


def head_kernel(
    n_glob, u_ref, b_ref, w_hbm, t_hbm,
    pb_hbm, pc_hbm, pd_hbm, du_ref, db_ref,
    w_s, t_s, z_s, ra_s, b_s, g_s, ut_s, m_s, s_s, ts_s, tz_s, stat_s, col_s, du_s, du_in,
    load_sem, stat_send, stat_recv, sib_send, sib_recv, far_sem, du_sem, out_sem, ready_sem,
):
    images, width = u_ref.shape
    classes = w_hbm.shape[1]
    padded = w_s.shape[1]
    chunk = 512
    n_chunks = padded // chunk
    tail = classes - (n_chunks - 1) * chunk
    part = width // 8
    half = images // 2

    vp = lax.axis_index("vp")
    dp = lax.axis_index("dp")
    core, x, y = lax.rem(dp, 2), lax.rem(dp // 2, 2), dp // 4
    p1 = jnp.where(core == 0, x, y)
    p2 = jnp.where(core == 0, y, x)
    sib = dp + 1 - 2 * core
    first = jnp.where(core == 0, dp + 2 - 4 * x, dp + 4 - 8 * y)
    z0 = lax.rem(vp, 2)
    near = vp + 1 - 2 * z0
    vp_size = stat_s.shape[0]
    others = [lax.rem(vp + k, vp_size) for k in range(1, vp_size)]

    barrier = pltpu.get_barrier_semaphore()
    for who in [(o, dp) for o in others] + [(vp, sib), (vp, first)]:
        pl.semaphore_signal(barrier, inc=1, device_id=who, device_id_type=MESH)

    def loads(i, n):
        cols = pl.ds(pl.multiple_of(i * chunk, chunk), n)
        return (
            pltpu.make_async_copy(w_hbm.at[:, cols], w_s.at[:, cols], load_sem.at[0, i]),
            pltpu.make_async_copy(t_hbm.at[:, cols], t_s.at[pl.ds(0, images), cols], load_sem.at[1, i]),
        )

    ahead = min(4, n_chunks - 1)
    for i in range(ahead):
        for c in loads(i, chunk):
            c.start()
    if padded > classes:
        b_s[:, classes:] = jnp.zeros((1, padded - classes), F32)
        w_s[:, classes:] = jnp.zeros((width, padded - classes), BF16)
        t_s[:, classes:] = jnp.zeros((t_s.shape[0], padded - classes), F32)
    b_s[:, :classes] = b_ref[...]
    m_s[...] = jnp.full_like(m_s, -jnp.inf)
    s_s[...] = jnp.zeros_like(s_s)
    ts_s[...] = jnp.zeros_like(ts_s)
    tz_s[...] = jnp.zeros_like(tz_s)
    limit = jnp.minimum(classes, NUM_CLASSES - vp * classes)

    def logits(i, carry):
        @pl.when(i + ahead < n_chunks - 1)
        def _():
            for c in loads(i + ahead, chunk):
                c.start()

        @pl.when(i + ahead == n_chunks - 1)
        def _():
            for c in loads(n_chunks - 1, tail):
                c.start()

        @pl.when(i < n_chunks - 1)
        def _():
            for c in loads(i, chunk):
                c.wait()

        @pl.when(i == n_chunks - 1)
        def _():
            for c in loads(n_chunks - 1, tail):
                c.wait()

        cols = pl.ds(pl.multiple_of(i * chunk, chunk), chunk)
        z = jnp.dot(u_ref[...], w_s[:, cols], preferred_element_type=F32) + b_s[:, cols]
        valid = i * chunk + lax.broadcasted_iota(jnp.int32, (1, chunk), 1) < limit
        t = t_s[:images, cols]
        tz = t * jnp.where(valid, z, 0.0)
        z = jnp.where(valid, z, -jnp.inf)
        z_s[:images, cols] = z
        parts = [slice(k, k + 128) for k in range(0, chunk, 128)]
        m_old = m_s[...]
        m_new = m_old
        for p in parts:
            m_new = jnp.maximum(m_new, z[:, p])
        base = jnp.where(m_new == -jnp.inf, 0.0, m_new)
        s = s_s[...] * jnp.exp(m_old - base)
        ts = ts_s[...]
        tzs = tz_s[...]
        for p in parts:
            s += jnp.exp(z[:, p] - base)
            ts += t[:, p]
            tzs += tz[:, p]
        m_s[...] = m_new
        s_s[...] = s
        ts_s[...] = ts
        tz_s[...] = tzs
        return carry

    lax.fori_loop(0, n_chunks, logits, 0)

    m = m_s[...].max(axis=1, keepdims=True)
    s = (s_s[...] * jnp.exp(m_s[...] - m)).sum(axis=1, keepdims=True)
    ts = ts_s[...].sum(axis=1, keepdims=True)
    tz = tz_s[...].sum(axis=1, keepdims=True)
    lane = lax.broadcasted_iota(jnp.int32, m_s.shape, 1)
    packed = jnp.where(lane == 0, m, jnp.where(lane == 1, s, jnp.where(lane == 2, ts, tz)))
    stat_s[vp] = packed.T[:8]

    pl.semaphore_wait(barrier, vp_size + 1)
    copies = []
    for k, o in enumerate(others):
        c = pltpu.make_async_remote_copy(
            src_ref=stat_s.at[vp], dst_ref=stat_s.at[vp], send_sem=stat_send.at[k], recv_sem=stat_recv.at[k],
            device_id=(o, dp), device_id_type=MESH,
        )
        c.start()
        copies.append(c)
    ut_s[...] = u_ref[...].T
    for c in copies:
        c.wait()

    stat = [stat_s[k] for k in range(vp_size)]
    m = functools.reduce(jnp.maximum, [a[0:1] for a in stat])
    s = sum(a[1:2] * jnp.exp(a[0:1] - m) for a in stat)
    ts = sum(a[2:3] for a in stat)
    tz = sum(a[3:4] for a in stat)
    log_norm = m + jnp.log(s)
    loss = (log_norm * ts - tz).sum(axis=1, keepdims=True)
    row = lax.broadcasted_iota(jnp.int32, (128, m.shape[1]), 0)
    col_s[...] = jnp.where(row == 0, log_norm, ts).T

    def grads(i, carry):
        cols = pl.ds(pl.multiple_of(i * chunk, chunk), chunk)
        g = (jnp.exp(z_s[:images, cols] - col_s[:, 0:1]) * col_s[:, 1:2] - t_s[:images, cols]) * (1.0 / n_glob)
        g_s[:, cols] = g.astype(BF16)
        db_ref[:, cols] = g.sum(axis=0, keepdims=True)
        return carry

    lax.fori_loop(0, n_chunks, grads, 0)
    db_ref[:, classes:] = loss + jnp.zeros((1, padded - classes), F32)

    pl.semaphore_signal(ready_sem, inc=1, device_id=(vp, sib), device_id_type=MESH)

    def dots(src, n, dst, add):
        left = ut_s[pl.ds(pl.multiple_of(src * part, part), n), :]

        def body(i, carry):
            cols = pl.ds(pl.multiple_of(i * chunk, chunk), chunk)
            v = jnp.dot(left, g_s[:, cols], preferred_element_type=F32)
            at = pl.ds(dst, n)
            if add:
                t_s[at, cols] = t_s[at, cols] + v
            else:
                z_s[at, cols] = v
            return carry

        lax.fori_loop(0, n_chunks, body, 0)

    def to_sibling(k, at):
        rows = pl.ds(pl.multiple_of(at * part, part), part)
        return pltpu.make_async_remote_copy(
            src_ref=z_s.at[rows, pl.ds(0, classes)], dst_ref=t_s.at[pl.ds(k * part, part), pl.ds(0, classes)],
            send_sem=sib_send.at[k], recv_sem=sib_recv.at[k], device_id=(vp, sib), device_id_type=MESH,
        )

    dots(4 * (1 - core) + 2 * (1 - p2), 2 * part, 0, False)
    sends = [to_sibling(0, 1 - p1), to_sibling(1, p1), to_sibling(2, 3 - p1), to_sibling(3, 2 + p1)]
    pl.semaphore_wait(ready_sem, 1)
    sends[0].start()
    dots(4 * (1 - core) + 2 * p2, 2 * part, 2 * part, False)
    sends[1].start()

    own = [4 * core + 2 * a + b for a, b in ((1 - p1, 1 - p2), (1 - p1, p2), (p1, 1 - p2), (p1, p2))]

    def piece(k):
        return t_s.at[pl.ds(k * part, part), pl.ds(0, classes)]

    sends[0].wait_recv()
    sends[2].start()
    sends[3].start()
    dots(own[0], part, 0, True)
    far = pltpu.make_async_remote_copy(
        src_ref=piece(0), dst_ref=ra_s, send_sem=far_sem.at[0], recv_sem=far_sem.at[1],
        device_id=(vp, first), device_id_type=MESH,
    )
    far.start()

    def du_dot(i, carry):
        cols = pl.ds(pl.multiple_of(i * chunk, chunk), chunk)
        v = lax.dot_general(g_s[:, cols], w_s[:, cols], (((1,), (1,)), ((), ())), preferred_element_type=F32)
        du_s[...] = du_s[...] + v
        return carry

    du_s[...] = jnp.zeros_like(du_s)
    lax.fori_loop(0, n_chunks, du_dot, 0)
    keep = pl.ds(pl.multiple_of(z0 * half, half), half)
    give = pl.ds(pl.multiple_of((1 - z0) * half, half), half)
    du_copy = pltpu.make_async_remote_copy(
        src_ref=du_s.at[give], dst_ref=du_in, send_sem=du_sem.at[0], recv_sem=du_sem.at[1],
        device_id=(near, dp), device_id_type=MESH,
    )
    du_copy.start()

    outs = []
    for k, out in ((1, pb_hbm), (2, pc_hbm), (3, pd_hbm)):
        sends[k].wait_recv()
        dots(own[k], part, k * part, True)
        c = pltpu.make_async_copy(piece(k), out, out_sem.at[k - 1])
        if k != 2:
            c.start()
        outs.append(c)
    for c in sends:
        c.wait_send()
    du_copy.wait()
    du_ref[...] = du_s[keep, :] + du_in[...]
    far.wait()

    def add_far(i, carry):
        cols = pl.ds(pl.multiple_of(i * 128, 128), 128)
        at = pl.ds(2 * part, part)
        t_s[at, cols] = t_s[at, cols] + ra_s[:, cols]
        return carry

    lax.fori_loop(0, classes // 128, add_far, 0)
    outs[1].start()
    for c in outs:
        c.wait()


def head(u, b, w, t, n_glob, vp_size):
    images, width = u.shape
    classes = w.shape[1]
    padded = (classes // 512 + 1) * 512
    part = width // 8
    rows = max(images, 4 * part)
    any_spec = pl.BlockSpec(memory_space=pl.ANY)
    vmem = pl.BlockSpec(memory_space=pltpu.VMEM)
    dma = pltpu.SemaphoreType.DMA
    piece = jax.ShapeDtypeStruct((part, classes), F32)
    return pl.pallas_call(
        functools.partial(head_kernel, n_glob),
        in_specs=[vmem, vmem, any_spec, any_spec],
        out_specs=[any_spec] * 3 + [vmem] * 2,
        out_shape=[piece] * 3 + [
            jax.ShapeDtypeStruct((images // 2, width), F32),
            jax.ShapeDtypeStruct((1, padded), F32),
        ],
        scratch_shapes=[
            pltpu.VMEM((width, padded), BF16),
            pltpu.VMEM((rows, padded), F32),
            pltpu.VMEM((rows, padded), F32),
            pltpu.VMEM((part, classes), F32),
            pltpu.VMEM((1, padded), F32),
            pltpu.VMEM((images, padded), BF16),
            pltpu.VMEM((width, images), BF16),
        ] + [pltpu.VMEM((images, 128), F32)] * 4 + [
            pltpu.VMEM((vp_size, 8, images), F32),
            pltpu.VMEM((images, 128), F32),
            pltpu.VMEM((images, width), F32),
            pltpu.VMEM((images // 2, width), F32),
            dma((2, padded // 512)),
            dma((vp_size - 1,)),
            dma((vp_size - 1,)),
            dma((4,)),
            dma((4,)),
            dma((2,)),
            dma((2,)),
            dma((3,)),
            pltpu.SemaphoreType.REGULAR,
        ],
        compiler_params=pltpu.CompilerParams(
            collective_id=0, has_side_effects=True, vmem_limit_bytes=60 * 1024 * 1024
        ),
        cost_estimate=pl.CostEstimate(
            flops=6 * images * width * classes, bytes_accessed=20 * width * classes, transcendentals=0
        ),
        name="head",
    )(u, b[None], w, t)


def solution(mesh):
    dp_size = mesh.shape["dp"]
    vp_size = mesh.shape["vp"]
    sibling = [(i, i ^ 1) for i in range(8)]
    along_x = [(i, i ^ 2) for i in range(8)]
    along_y = [(i, i ^ 4) for i in range(8)]
    first = [(i, i ^ (4 if i & 1 else 2)) for i in range(8)]
    second = [(i, i ^ (2 if i & 1 else 4)) for i in range(8)]
    near = [(i, i ^ 1) for i in range(vp_size)]
    distant = [(i, i ^ 2) for i in range(vp_size)]

    def local_step(h_loc, gamma, beta, w_loc, b_loc, t_loc):
        images, _, width = h_loc.shape
        n_glob = images * dp_size
        classes = w_loc.shape[1]
        part = width // 8
        quarter = images // 4
        dp = lax.axis_index("dp")
        vp = lax.axis_index("vp")
        core, x, y = dp & 1, (dp >> 1) & 1, dp >> 2
        z0, z1 = vp & 1, vp >> 1
        p1 = jnp.where(core == 0, x, y)
        p2 = jnp.where(core == 0, y, x)
        own = [4 * core + 2 * a + b for a, b in ((1 - p1, 1 - p2), (1 - p1, p2), (p1, 1 - p2), (p1, p2))]
        sib = [4 * (1 - core) + 2 * a + b for a, b in ((1 - p2, 1 - p1), (1 - p2, p1), (p2, 1 - p1), (p2, p1))]

        ht = h_loc.transpose(1, 0, 2)
        u = pool_forward(ht, gamma, beta)
        b, c, d, du_half, db = head(u, b_loc, w_loc, t_loc, n_glob, vp_size)

        def send(v, pairs):
            return lax.ppermute(v, "dp", pairs)

        r_d = send(b, first)
        r_d2 = send(c, second)

        got = lax.ppermute(lax.dynamic_slice(du_half, ((1 - z1) * quarter, 0), (quarter, width)), "vp", distant)
        du_own = lax.dynamic_slice(du_half, (z1 * quarter, 0), (quarter, width)) + got
        du_far = lax.ppermute(du_own, "vp", distant)
        du_near = lax.ppermute(du_own, "vp", near)
        du_last = lax.ppermute(du_far, "vp", near)

        for pairs in (sibling, along_x, along_y):
            db = db + send(db, pairs)

        dh, token = pool_backward(ht, du_own, gamma, None, 2 * z0 + z1, db)
        dh, token = pool_backward(ht, du_far, gamma, dh, 2 * z0 + 1 - z1, token)
        d = add_after(d, r_d, r_d2, token, du_near)
        c_fin = send(d, second)
        b_fin = send(d, first)
        dh, token = pool_backward(ht, du_near, gamma, dh, 2 * (1 - z0) + z1, d)
        dh, token = pool_backward(ht, du_last, gamma, dh, 2 * (1 - z0) + 1 - z1, token)
        a_fin = send(c_fin, first)
        mine = [a_fin, b_fin, c_fin, d]
        theirs = [send(v, sibling) for v in mine]

        out = place_first(d, own[3], width)
        for v, k in ((theirs[3], sib[3]), (mine[2], own[2]), (theirs[2], sib[2]),
                     (mine[1], own[1]), (theirs[1], sib[1]), (mine[0], own[0]), (theirs[0], sib[0])):
            out = lax.dynamic_update_slice(out, v, (k * part, 0))
        return db[0, classes] / n_glob, out, db[0, :classes], dh.transpose(1, 0, 2)

    return jax.shard_map(
        local_step,
        mesh=mesh,
        in_specs=(P("dp", None, None), P(), P(), P(None, "vp"), P("vp"), P("dp", "vp")),
        out_specs=(P(), P(None, "vp"), P("vp"), P("dp", None, None)),
        check_vma=False,
    )
```

profile of v0, /device:TPU:0, one launch (start us, length us, event | category | flops | bytes accessed | tf_op | source)
XLA Modules:
  0.0 343.2 jit_solution(11965081323240333210)
XLA Ops:
  2.0 35.1 %pool_forward.1.u_ref = bf16[512,1024]{1,0:T(8,128)(2,1)} custom-call(bf16[49,512,1024]{2,1,0:T(8,128)(2,1)} %bitcast.10, f32[1,1024]{1,0:T(1,128)} %bitcast.16, f32[1,1024]{1,0:T(1,128)} %bitcast.21), custom_call_target="tpu_custom_call" | custom-call | flops 8220835840 | bytes 51380224 | tf_op jit(solution)/shard_map/pool_forward/pallas_call | solution.py:44
  37.1 71.9 %head.1 = (f32[128,5504]{1,0:T(8,128)}, f32[128,5504]{1,0:T(8,128)}, f32[128,5504]{1,0:T(8,128)}, f32[256,1024]{1,0:T(8,128)}, f32[1,5632]{1,0:T(1,128)}) custom-call(bf16[512,1024]{1,0:T(8,128)(2,1)} %pool_forward.1.u_ref, f32[1,5504]{1,0:T(1,128)} %broadcast_in_dim.30.b_ref, bf16[1024,5504]{1,0:T(8,128)(2,1)} %w_hbm.1, f32[512,5504]{1,0:T(8,128)} %t_hbm.1), custom_call_target="tpu_custom_call" | custom-call | flops 17314086912 | bytes 112721920 | tf_op jit(solution)/shard_map/head/pallas_call | solution.py:404
  109.8 1.5 collective-permute-start.4
  113.1 25.5 %collective-permute-done.5 = f32[128,1024]{1,0:T(8,128)} collective-permute-done((f32[128,1024]{1,0:T(8,128)S(1)}, f32[128,1024]{1,0:T(8,128)}, u32[]{:S(2)}, u32[]{:S(2)}) %collective-permute-start.5) | collective-permute-done | bytes 524320 | tf_op jit(solution)/shard_map/ppermute | solution.py:481
  143.1 30.2 %collective-permute-done.1 = f32[1,5632]{1,0:T(1,128)S(1)} collective-permute-done((f32[1,5632]{1,0:T(1,128)S(1)}, f32[1,5632]{1,0:T(1,128)S(1)}, u32[]{:S(2)}, u32[]{:S(2)}) %collective-permute-start.1) | collective-permute-done | bytes 22560 | tf_op jit(solution)/shard_map/ppermute | solution.py:476
  173.3 1.9 collective-permute-start.2
  175.2 2.0 collective-permute-done.2
  178.3 16.1 %pool_backward.4 = (bf16[49,512,1024]{2,1,0:T(8,128)(2,1)}, f32[8,128]{1,0:T(8,128)}) custom-call(s32[1]{0:T(128)} %bitcast.6.off_ref, bf16[49,512,1024]{2,1,0:T(8,128)(2,1)} %bitcast.11, f32[128,1024]{1,0:T(8,128)} %copy-done.1, f32[1,1024]{1,0:T(1,128)} %bitcast.17, f32[1,5632]{1,0:T(1,128)} %add.93.rest_0_), custom_call_target="tpu_custom_call" | custom-call | flops 3082813440 | bytes 25690112 | tf_op jit(solution)/shard_map/pool_backward/pallas_call | solution.py:99
  194.4 16.1 %pool_backward.5 = (bf16[49,512,1024]{2,1,0:T(8,128)(2,1)}, f32[8,128]{1,0:T(8,128)}) custom-call(s32[1]{0:T(128)} %bitcast.5.off_ref, bf16[49,512,1024]{2,1,0:T(8,128)(2,1)} %bitcast.12, f32[128,1024]{1,0:T(8,128)} %collective-permute-done.6.du_ref, f32[1,1024]{1,0:T(1,128)} %bitcast.18, ...), custom_call_target="tpu_custom_call", output_to_operand_aliasing={{0}: (5, {})} | custom-call | flops 3082813440 | bytes 25690112 | tf_op jit(solution)/shard_map/pool_backward/pallas_call | solution.py:99
  210.6 1.5 copy-done
  212.1 5.4 %add_after.1.v_ref.rest_0_ = f32[128,5504]{1,0:T(8,128)} custom-call(f32[128,5504]{1,0:T(8,128)} %get-tuple-element.17.a_ref, f32[128,5504]{1,0:T(8,128)} %copy-done, f32[128,5504]{1,0:T(8,128)} %collective-permute-done.4.c_ref, f32[8,128]{1,0:T(8,128)} %get-tuple-element.23.rest_0_, f32[128,1024]{1,0:T(8,128)} %collective-permute-done.7.rest_1_.du_ref), custom_call_target="tpu_custom_call" | custom-call | flops 7045120 | bytes 11272192 | tf_op jit(solution)/shard_map/add_after/pallas_call | solution.py:131
  217.5 2.0 collective-permute-start.9
  220.9 60.7 %collective-permute-done.9 = f32[128,5504]{1,0:T(8,128)} collective-permute-done((f32[128,5504]{1,0:T(8,128)}, f32[128,5504]{1,0:T(8,128)}, u32[]{:S(2)}, u32[]{:S(2)}) %collective-permute-start.9) | collective-permute-done | bytes 2818080 | tf_op jit(solution)/shard_map/ppermute | solution.py:476
  281.7 1.6 collective-permute-start.15
  285.1 4.1 %place_first.1 = f32[1024,5504]{1,0:T(8,128)} custom-call(s32[1]{0:T(128)} %bitcast.4.off_ref, f32[128,5504]{1,0:T(8,128)} %add_after.1.v_ref.rest_0_), custom_call_target="tpu_custom_call" | custom-call | flops 7045120 | bytes 5636096 | tf_op jit(solution)/shard_map/place_first/pallas_call | solution.py:149
  289.1 16.1 %pool_backward.6 = (bf16[49,512,1024]{2,1,0:T(8,128)(2,1)}, f32[8,128]{1,0:T(8,128)}) custom-call(s32[1]{0:T(128)} %bitcast.8.off_ref, bf16[49,512,1024]{2,1,0:T(8,128)(2,1)} %bitcast.13, f32[128,1024]{1,0:T(8,128)} %collective-permute-done.7.rest_1_.du_ref, f32[1,1024]{1,0:T(1,128)} %bitcast.19, ...), custom_call_target="tpu_custom_call", output_to_operand_aliasing={{0}: (5, {})} | custom-call | flops 3082813440 | bytes 25690112 | tf_op jit(solution)/shard_map/pool_backward/pallas_call | solution.py:99
  306.0 16.1 %pool_backward.7 = (bf16[49,512,1024]{2,1,0:T(8,128)(2,1)}, f32[8,128]{1,0:T(8,128)}) custom-call(s32[1]{0:T(128)} %bitcast.7.off_ref, bf16[49,512,1024]{2,1,0:T(8,128)(2,1)} %bitcast.14, f32[128,1024]{1,0:T(8,128)} %copy-done.2, f32[1,1024]{1,0:T(1,128)} %bitcast.20, f32[8,128]{1,0:T(8,128)} %get-tuple-element.25.rest_0_, ...), custom_call_target="tpu_custom_call", output_to_operand_aliasing={{0}: (5, {})} | custom-call | flops 3082813440 | bytes 25690112 | tf_op jit(solution)/shard_map/pool_backward/pallas_call | solution.py:99
  322.4 3.5 %constant_dynamic-update-slice_fusion.6 = f32[1024,5504]{1,0:T(8,128)} fusion(f32[1024,5504]{1,0:T(8,128)} %place_first.1, f32[128,5504]{1,0:T(8,128)} %collective-permute-done.8, s32[]{:T(128)S(6)} %select_n.38), kind=kLoop, calls=%fused_computation.8 | loop fusion | bytes 5636100 | tf_op jit(solution)/shard_map/dynamic_update_slice | solution.py:504
  325.9 3.5 %constant_dynamic-update-slice_fusion.5 = f32[1024,5504]{1,0:T(8,128)} fusion(f32[1024,5504]{1,0:T(8,128)} %constant_dynamic-update-slice_fusion.6, f32[128,5504]{1,0:T(8,128)} %collective-permute-done.9, s32[]{:T(128)S(6)} %select_n.39), kind=kLoop, calls=%fused_computation.7 | loop fusion | bytes 5636100 | tf_op jit(solution)/shard_map/dynamic_update_slice | solution.py:504
  329.7 3.5 %constant_dynamic-update-slice_fusion.4 = f32[1024,5504]{1,0:T(8,128)} fusion(f32[1024,5504]{1,0:T(8,128)} %constant_dynamic-update-slice_fusion.5, f32[128,5504]{1,0:T(8,128)} %collective-permute-done.10, s32[]{:T(128)S(6)} %select_n.40), kind=kLoop, calls=%fused_computation.6 | loop fusion | bytes 5636100 | tf_op jit(solution)/shard_map/dynamic_update_slice | solution.py:504
  333.3 1.7 constant_dynamic-update-slice_fusion.3
  335.0 1.7 constant_dynamic-update-slice_fusion.2
  336.8 3.5 %constant_dynamic-update-slice_fusion.1 = f32[1024,5504]{1,0:T(8,128)} fusion(f32[1024,5504]{1,0:T(8,128)} %constant_dynamic-update-slice_fusion.2, f32[128,5504]{1,0:T(8,128)} %collective-permute-done.13, s32[]{:T(128)S(6)} %select_n.43), kind=kLoop, calls=%fused_computation.3 | loop fusion | bytes 5636100 | tf_op jit(solution)/shard_map/dynamic_update_slice | solution.py:504
  340.3 1.7 constant_dynamic-update-slice_fusion
  (39 shorter events, 13.6 us)
Async XLA Ops:
  109.0 101.5 %collective-permute-start.3 = (f32[128,5504]{1,0:T(8,128)}, f32[128,5504]{1,0:T(8,128)S(1)}, u32[]{:S(2)}, u32[]{:S(2)}) collective-permute-start(f32[128,5504]{1,0:T(8,128)} %get-tuple-element.18), channel_id=1, source_target_pairs={{0,2},{1,5},{2,0},{3,7},{4,6},{5,1},{6,4},{7,3},{8,10},{9,13},{10,... | collective-permute-start | bytes 8454152 | tf_op jit(solution)/shard_map/ppermute | solution.py:476
  109.8 100.7 %collective-permute-start.4 = (f32[128,5504]{1,0:T(8,128)}, f32[128,5504]{1,0:T(8,128)}, u32[]{:S(2)}, u32[]{:S(2)}) collective-permute-start(f32[128,5504]{1,0:T(8,128)} %get-tuple-element.19), channel_id=1, source_target_pairs={{0,4},{1,3},{2,6},{3,1},{4,0},{5,7},{6,2},{7,5},{8,12},{9,11},{10,... | collective-permute-start | bytes 8454152 | tf_op jit(solution)/shard_map/ppermute | solution.py:476
  112.4 26.2 %collective-permute-start.5 = (f32[128,1024]{1,0:T(8,128)S(1)}, f32[128,1024]{1,0:T(8,128)}, u32[]{:S(2)}, u32[]{:S(2)}) collective-permute-start(f32[128,1024]{1,0:T(8,128)S(1)} %constant_dynamic-slice_fusion), channel_id=1, source_target_pairs={{0,16},{8,24},{16,0},{24,8},{1,17},{9,25},{17,1},{25,9},{2,18},{10... | collective-permute-start | bytes 1572872 | tf_op jit(solution)/shard_map/ppermute | solution.py:481
  139.8 38.5 %copy-start.1 = (f32[128,1024]{1,0:T(8,128)}, f32[128,1024]{1,0:T(8,128)S(1)}, u32[]{:S(2)}) copy-start(f32[128,1024]{1,0:T(8,128)S(1)} %dynamic-slice_add_fusion.du_ref) | copy-start | bytes 1572868
  139.8 54.6 %collective-permute-start.6 = (f32[128,1024]{1,0:T(8,128)S(1)}, f32[128,1024]{1,0:T(8,128)}, u32[]{:S(2)}, u32[]{:S(2)}) collective-permute-start(f32[128,1024]{1,0:T(8,128)S(1)} %dynamic-slice_add_fusion.du_ref), channel_id=1, source_target_pairs={{0,16},{8,24},{16,0},{24,8},{1,17},{9,25},{17,1},{25,9},{2,18},{10... | collective-permute-start | bytes 1572872 | tf_op jit(solution)/shard_map/ppermute | solution.py:483
  139.9 1.5 collective-permute-start
  142.2 31.1 %collective-permute-start.1 = (f32[1,5632]{1,0:T(1,128)S(1)}, f32[1,5632]{1,0:T(1,128)S(1)}, u32[]{:S(2)}, u32[]{:S(2)}) collective-permute-start(f32[1,5632]{1,0:T(1,128)S(1)} %add.91), channel_id=1, source_target_pairs={{0,2},{1,3},{2,0},{3,1},{4,6},{5,7},{6,4},{7,5},{8,10},{9,11},{10,... | collective-permute-start | bytes 67592 | tf_op jit(solution)/shard_map/ppermute | solution.py:476
  173.3 3.9 %collective-permute-start.2 = (f32[1,5632]{1,0:T(1,128)S(1)}, f32[1,5632]{1,0:T(1,128)S(1)}, u32[]{:S(2)}, u32[]{:S(2)}) collective-permute-start(f32[1,5632]{1,0:T(1,128)S(1)} %add.92), channel_id=1, source_target_pairs={{0,4},{1,5},{2,6},{3,7},{4,0},{5,1},{6,2},{7,3},{8,12},{9,13},{10,... | collective-permute-start | bytes 67592 | tf_op jit(solution)/shard_map/ppermute | solution.py:476
  177.8 32.7 %collective-permute-start.7 = (f32[128,1024]{1,0:T(8,128)S(1)}, f32[128,1024]{1,0:T(8,128)}, u32[]{:S(2)}, u32[]{:S(2)}) collective-permute-start(f32[128,1024]{1,0:T(8,128)S(1)} %dynamic-slice_add_fusion.du_ref), channel_id=1, source_target_pairs={{0,8},{8,0},{16,24},{24,16},{1,9},{9,1},{17,25},{25,17},{2,10},{10... | collective-permute-start | bytes 1572872 | tf_op jit(solution)/shard_map/ppermute | solution.py:484
  194.4 88.8 %copy-start.3 = (f32[1,5632]{1,0:T(1,128)S(1)}, f32[1,5632]{1,0:T(1,128)}, u32[]{:S(2)}) copy-start(f32[1,5632]{1,0:T(1,128)} %add.93.rest_0_) | copy-start | bytes 67588
  210.5 1.6 copy-start
  217.5 64.2 %collective-permute-start.9 = (f32[128,5504]{1,0:T(8,128)}, f32[128,5504]{1,0:T(8,128)}, u32[]{:S(2)}, u32[]{:S(2)}) collective-permute-start(f32[128,5504]{1,0:T(8,128)} %add_after.1.v_ref.rest_0_), channel_id=1, source_target_pairs={{0,4},{1,3},{2,6},{3,1},{4,0},{5,7},{6,2},{7,5},{8,12},{9,11},{10,... | collective-permute-start | bytes 8454152 | tf_op jit(solution)/shard_map/ppermute | solution.py:476
  219.5 102.6 %collective-permute-start.11 = (f32[128,5504]{1,0:T(8,128)}, f32[128,5504]{1,0:T(8,128)S(1)}, u32[]{:S(2)}, u32[]{:S(2)}) collective-permute-start(f32[128,5504]{1,0:T(8,128)} %add_after.1.v_ref.rest_0_), channel_id=1, source_target_pairs={{0,2},{1,5},{2,0},{3,7},{4,6},{5,1},{6,4},{7,3},{8,10},{9,13},{10,... | collective-permute-start | bytes 8454152 | tf_op jit(solution)/shard_map/ppermute | solution.py:476
  220.9 101.5 %collective-permute-start.8 = (f32[128,5504]{1,0:T(8,128)}, f32[128,5504]{1,0:T(8,128)}, u32[]{:S(2)}, u32[]{:S(2)}) collective-permute-start(f32[128,5504]{1,0:T(8,128)} %add_after.1.v_ref.rest_0_), channel_id=1, source_target_pairs={{0,1},{1,0},{2,3},{3,2},{4,5},{5,4},{6,7},{7,6},{8,9},{9,8},{10,11... | collective-permute-start | bytes 8454152 | tf_op jit(solution)/shard_map/ppermute | solution.py:476
  281.6 47.8 %collective-permute-start.13 = (f32[128,5504]{1,0:T(8,128)}, f32[128,5504]{1,0:T(8,128)}, u32[]{:S(2)}, u32[]{:S(2)}) collective-permute-start(f32[128,5504]{1,0:T(8,128)} %collective-permute-done.9), channel_id=1, source_target_pairs={{0,2},{1,5},{2,0},{3,7},{4,6},{5,1},{6,4},{7,3},{8,10},{9,13},{10,... | collective-permute-start | bytes 8454152 | tf_op jit(solution)/shard_map/ppermute | solution.py:476
  281.7 48.1 %collective-permute-start.10 = (f32[128,5504]{1,0:T(8,128)}, f32[128,5504]{1,0:T(8,128)}, u32[]{:S(2)}, u32[]{:S(2)}) collective-permute-start(f32[128,5504]{1,0:T(8,128)} %collective-permute-done.9), channel_id=1, source_target_pairs={{0,1},{1,0},{2,3},{3,2},{4,5},{5,4},{6,7},{7,6},{8,9},{9,8},{10,11... | collective-permute-start | bytes 8454152 | tf_op jit(solution)/shard_map/ppermute | solution.py:476
  281.7 23.6 %collective-permute-start.15 = (f32[128,1024]{1,0:T(8,128)}, f32[128,1024]{1,0:T(8,128)S(1)}, u32[]{:S(2)}, u32[]{:S(2)}) collective-permute-start(f32[128,1024]{1,0:T(8,128)} %collective-permute-done.6.du_ref), channel_id=1, source_target_pairs={{0,8},{8,0},{16,24},{24,16},{1,9},{9,1},{17,25},{25,17},{2,10},{10... | collective-permute-start | bytes 1572872 | tf_op jit(solution)/shard_map/ppermute | solution.py:485
  305.2 0.8 copy-start.2
  322.1 12.9 %collective-permute-start.12 = (f32[128,5504]{1,0:T(8,128)S(1)}, f32[128,5504]{1,0:T(8,128)S(1)}, u32[]{:S(2)}, u32[]{:S(2)}) collective-permute-start(f32[128,5504]{1,0:T(8,128)S(1)} %collective-permute-done.11), channel_id=1, source_target_pairs={{0,1},{1,0},{2,3},{3,2},{4,5},{5,4},{6,7},{7,6},{8,9},{9,8},{10,11... | collective-permute-start | bytes 8454152 | tf_op jit(solution)/shard_map/ppermute | solution.py:476
  329.5 10.8 %collective-permute-start.14 = (f32[128,5504]{1,0:T(8,128)}, f32[128,5504]{1,0:T(8,128)S(1)}, u32[]{:S(2)}, u32[]{:S(2)}) collective-permute-start(f32[128,5504]{1,0:T(8,128)} %collective-permute-done.13), channel_id=1, source_target_pairs={{0,1},{1,0},{2,3},{3,2},{4,5},{5,4},{6,7},{7,6},{8,9},{9,8},{10,11... | collective-permute-start | bytes 8454152 | tf_op jit(solution)/shard_map/ppermute | solution.py:476
where the time goes:
time: 344 us; the launch traced here: 343 us
  Pallas kernels  181 us (53%)
  waiting for transfers between devices  120 us (35%)
  local copies, waits for them, and re-layouts  25.3 us (7%)
  starting transfers between devices  12.1 us (4%)
    ppermute x12, waiting for transfers between devices, send(): return lax.ppermute(v, 'dp', pairs)  94.3 us
    pallas_call x1, Pallas kernels, head(): pl.pallas_call(functools.partial(head_kernel, n_glob), in_specs=[vmem, vm...  71.9 us
    pallas_call x4, Pallas kernels, pool_backward(): pl.pallas_call(pool_backward_kernel, grid_spec=pltpu.PrefetchScalarGridSp...  64.3 us
    pallas_call x1, Pallas kernels, pool_forward(): pl.pallas_call(pool_kernel, grid=(images // rows,), in_specs=[pl.BlockSpe...  35.1 us
    ppermute x1, waiting for transfers between devices, local_step(): lax.ppermute(lax.dynamic_slice(du_half, ((1 - z1) * quarter, 0), (quarter...  25.5 us
    dynamic_update_slice x7, local copies, waits for them, and re-layouts, local_step(): out = lax.dynamic_update_slice(out, v, (k * part, 0))  19.3 us
    ppermute x12, starting transfers between devices, send(): return lax.ppermute(v, 'dp', pairs)  9.21 us
  transfers between devices with their start and end apart: 16, of which 5 were waited for; matrix products, arithmetic and copies ran while one was open for 7% of the time, Pallas kernels for 20%

commit v1 on v0

--- a/solution.py
+++ b/solution.py
@@ -121,24 +121,6 @@
     )(*args)
 
 
-def add_kernel(a_ref, b_ref, c_ref, *rest):
-    rest[-1][...] = (a_ref[...] + b_ref[...]) + c_ref[...]
-
-
-def add_after(a, b, c, *after, rows=32):
-    n = a.shape[1]
-    spec = pl.BlockSpec((rows, n), lambda i: (i, 0))
-    return pl.pallas_call(
-        add_kernel,
-        grid=(a.shape[0] // rows,),
-        in_specs=[spec] * 3 + [pl.BlockSpec(memory_space=pl.ANY)] * len(after),
-        out_specs=spec,
-        out_shape=jax.ShapeDtypeStruct(a.shape, a.dtype),
-        cost_estimate=pl.CostEstimate(flops=10 * a.size, bytes_accessed=16 * a.size, transcendentals=0),
-        name="add_after",
-    )(a, b, c, *after)
-
-
 def place_kernel(off_ref, v_ref, o_ref):
     o_ref[...] = v_ref[...]
 
@@ -163,8 +145,8 @@
 def head_kernel(
     n_glob, u_ref, b_ref, w_hbm, t_hbm,
     pb_hbm, pc_hbm, pd_hbm, du_ref, db_ref,
-    w_s, t_s, z_s, ra_s, b_s, g_s, ut_s, m_s, s_s, ts_s, tz_s, stat_s, col_s, du_s, du_in,
-    load_sem, stat_send, stat_recv, sib_send, sib_recv, far_sem, du_sem, out_sem, ready_sem,
+    w_s, t_s, z_s, ra_s, b_s, db_s, g_s, ut_s, m_s, s_s, ts_s, tz_s, stat_s, col_s, du_s, du_in,
+    load_sem, stat_send, stat_recv, sib_send, sib_recv, far_sem, du_sem, db_send, db_recv, out_sem, ready_sem,
 ):
     images, width = u_ref.shape
     classes = w_hbm.shape[1]
@@ -181,14 +163,15 @@
     p1 = jnp.where(core == 0, x, y)
     p2 = jnp.where(core == 0, y, x)
     sib = dp + 1 - 2 * core
-    first = jnp.where(core == 0, dp + 2 - 4 * x, dp + 4 - 8 * y)
+    along_x, along_y = dp + 2 - 4 * x, dp + 4 - 8 * y
+    first = jnp.where(core == 0, along_x, along_y)
     z0 = lax.rem(vp, 2)
     near = vp + 1 - 2 * z0
     vp_size = stat_s.shape[0]
     others = [lax.rem(vp + k, vp_size) for k in range(1, vp_size)]
 
     barrier = pltpu.get_barrier_semaphore()
-    for who in [(o, dp) for o in others] + [(vp, sib), (vp, first)]:
+    for who in [(o, dp) for o in others] + [(vp, sib), (vp, along_x), (vp, along_y)]:
         pl.semaphore_signal(barrier, inc=1, device_id=who, device_id_type=MESH)
 
     def loads(i, n):
@@ -270,7 +253,7 @@
     packed = jnp.where(lane == 0, m, jnp.where(lane == 1, s, jnp.where(lane == 2, ts, tz)))
     stat_s[vp] = packed.T[:8]
 
-    pl.semaphore_wait(barrier, vp_size + 1)
+    pl.semaphore_wait(barrier, vp_size + 2)
     copies = []
     for k, o in enumerate(others):
         c = pltpu.make_async_remote_copy(
@@ -297,13 +280,31 @@
         cols = pl.ds(pl.multiple_of(i * chunk, chunk), chunk)
         g = (jnp.exp(z_s[:images, cols] - col_s[:, 0:1]) * col_s[:, 1:2] - t_s[:images, cols]) * (1.0 / n_glob)
         g_s[:, cols] = g.astype(BF16)
-        db_ref[:, cols] = g.sum(axis=0, keepdims=True)
+        db_s[0, :, cols] = g.sum(axis=0, keepdims=True)
         return carry
 
     lax.fori_loop(0, n_chunks, grads, 0)
-    db_ref[:, classes:] = loss + jnp.zeros((1, padded - classes), F32)
+    db_s[0, :, classes:] = loss + jnp.zeros((1, padded - classes), F32)
 
     pl.semaphore_signal(ready_sem, inc=1, device_id=(vp, sib), device_id_type=MESH)
+
+    def db_copy(k, who):
+        return pltpu.make_async_remote_copy(
+            src_ref=db_s.at[2 * k], dst_ref=db_s.at[2 * k + 1], send_sem=db_send.at[k], recv_sem=db_recv.at[k],
+            device_id=(vp, who), device_id_type=MESH,
+        )
+
+    db_copies = [db_copy(0, sib), db_copy(1, along_x), db_copy(2, along_y)]
+
+    def db_next(k):
+        db_copies[k].wait()
+        if k < 2:
+            db_s[2 * k + 2] = db_s[2 * k] + db_s[2 * k + 1]
+            db_copies[k + 1].start()
+        else:
+            db_ref[...] = db_s[4] + db_s[5]
+
+    db_copies[0].start()
 
     def dots(src, n, dst, add):
         left = ut_s[pl.ds(pl.multiple_of(src * part, part), n), :]
@@ -331,8 +332,10 @@
     sends = [to_sibling(0, 1 - p1), to_sibling(1, p1), to_sibling(2, 3 - p1), to_sibling(3, 2 + p1)]
     pl.semaphore_wait(ready_sem, 1)
     sends[0].start()
+    db_next(0)
     dots(4 * (1 - core) + 2 * p2, 2 * part, 2 * part, False)
     sends[1].start()
+    db_next(1)
 
     own = [4 * core + 2 * a + b for a, b in ((1 - p1, 1 - p2), (1 - p1, p2), (p1, 1 - p2), (p1, p2))]
 
@@ -364,6 +367,7 @@
         device_id=(near, dp), device_id_type=MESH,
     )
     du_copy.start()
+    db_next(2)
 
     outs = []
     for k, out in ((1, pb_hbm), (2, pc_hbm), (3, pd_hbm)):
@@ -415,6 +419,7 @@
             pltpu.VMEM((rows, padded), F32),
             pltpu.VMEM((part, classes), F32),
             pltpu.VMEM((1, padded), F32),
+            pltpu.VMEM((6, 1, padded), F32),
             pltpu.VMEM((images, padded), BF16),
             pltpu.VMEM((width, images), BF16),
         ] + [pltpu.VMEM((images, 128), F32)] * 4 + [
@@ -430,6 +435,8 @@
             dma((2,)),
             dma((2,)),
             dma((3,)),
+            dma((3,)),
+            dma((3,)),
             pltpu.SemaphoreType.REGULAR,
         ],
         compiler_params=pltpu.CompilerParams(
@@ -446,8 +453,6 @@
     dp_size = mesh.shape["dp"]
     vp_size = mesh.shape["vp"]
     sibling = [(i, i ^ 1) for i in range(8)]
-    along_x = [(i, i ^ 2) for i in range(8)]
-    along_y = [(i, i ^ 4) for i in range(8)]
     first = [(i, i ^ (4 if i & 1 else 2)) for i in range(8)]
     second = [(i, i ^ (2 if i & 1 else 4)) for i in range(8)]
     near = [(i, i ^ 1) for i in range(vp_size)]
@@ -484,12 +489,9 @@
         du_near = lax.ppermute(du_own, "vp", near)
         du_last = lax.ppermute(du_far, "vp", near)
 
-        for pairs in (sibling, along_x, along_y):
-            db = db + send(db, pairs)
-
-        dh, token = pool_backward(ht, du_own, gamma, None, 2 * z0 + z1, db)
+        dh, token = pool_backward(ht, du_own, gamma, None, 2 * z0 + z1, du_own)
         dh, token = pool_backward(ht, du_far, gamma, dh, 2 * z0 + 1 - z1, token)
-        d = add_after(d, r_d, r_d2, token, du_near)
+        d = ((d + r_d) + r_d2) + token[0, 0]
         c_fin = send(d, second)
         b_fin = send(d, first)
         dh, token = pool_backward(ht, du_near, gamma, dh, 2 * (1 - z0) + z1, d)

time: 344 us -> 314 us (0.913)
  waiting for transfers between devices: 120 us -> 96.3 us
  starting transfers between devices: 12.1 us -> 5 us
  Pallas kernels: 181 us -> 175 us
    ppermute x12 -> x9, waiting for transfers between devices: 94.3 us -> 62.8 us  [send(): return lax.ppermute(v, 'dp', pairs)]
    ppermute x1, waiting for transfers between devices: 0.01 us -> 7.99 us  [local_step(): du_far = lax.ppermute(du_own, 'vp', distant)]
    pallas_call x1 -> x0, Pallas kernels: 5.37 us -> none  [add_after(): pl.pallas_call(add_kernel, grid=(a.shape[0] // rows,), in_specs=[spec] *...]
    ppermute x12 -> x9, starting transfers between devices: 9.21 us -> 4.4 us  [send(): return lax.ppermute(v, 'dp', pairs)]
  transfers between devices with their start and end apart: 16 -> 13, of which waited for: 5 -> 3; matrix products, arithmetic and copies ran while one was open for 7% -> 8% of each run, Pallas kernels for 20% -> 22%
where the time goes in v1:
time: 314 us; the launch traced here: 313 us
  Pallas kernels  175 us (56%)
  waiting for transfers between devices  96.3 us (31%)
  local copies, waits for them, and re-layouts  28.4 us (9%)
  other arithmetic  5.62 us (2%)
  starting transfers between devices  5 us (2%)
    pallas_call x1, Pallas kernels, head(): pl.pallas_call(functools.partial(head_kernel, n_glob), in_specs=[vmem, vm...  71.8 us
    pallas_call x4, Pallas kernels, pool_backward(): pl.pallas_call(pool_backward_kernel, grid_spec=pltpu.PrefetchScalarGridSp...  64.5 us
    ppermute x9, waiting for transfers between devices, send(): return lax.ppermute(v, 'dp', pairs)  62.8 us
    pallas_call x1, Pallas kernels, pool_forward(): pl.pallas_call(pool_kernel, grid=(images // rows,), in_specs=[pl.BlockSpe...  35.1 us
    ppermute x1, waiting for transfers between devices, local_step(): lax.ppermute(lax.dynamic_slice(du_half, ((1 - z1) * quarter, 0), (quarter...  25.5 us
    dynamic_update_slice x7, local copies, waits for them, and re-layouts, local_step(): out = lax.dynamic_update_slice(out, v, (k * part, 0))  21.1 us
    ppermute x1, waiting for transfers between devices, local_step(): du_far = lax.ppermute(du_own, 'vp', distant)  7.99 us
  transfers between devices with their start and end apart: 13, of which 3 were waited for; matrix products, arithmetic and copies ran while one was open for 8% of the time, Pallas kernels for 22%

profile of v1, /device:TPU:0, one launch (start us, length us, event | category | flops | bytes accessed | tf_op | source)
XLA Modules:
  0.0 313.3 jit_solution(6189188112811794794)
XLA Ops:
  0.6 1.4 broadcast_in_dim.30.b_ref
  2.0 35.1 %pool_forward.1.u_ref = bf16[512,1024]{1,0:T(8,128)(2,1)} custom-call(bf16[49,512,1024]{2,1,0:T(8,128)(2,1)} %bitcast.11, f32[1,1024]{1,0:T(1,128)} %bitcast.17, f32[1,1024]{1,0:T(1,128)} %bitcast.22), custom_call_target="tpu_custom_call" | custom-call | flops 8220835840 | bytes 51380224 | tf_op jit(solution)/shard_map/pool_forward/pallas_call | solution.py:44
  37.1 71.8 %head.1 = (f32[128,5504]{1,0:T(8,128)}, f32[128,5504]{1,0:T(8,128)}, f32[128,5504]{1,0:T(8,128)}, f32[256,1024]{1,0:T(8,128)}, f32[1,5632]{1,0:T(1,128)}) custom-call(bf16[512,1024]{1,0:T(8,128)(2,1)} %pool_forward.1.u_ref, f32[1,5504]{1,0:T(1,128)} %broadcast_in_dim.30.b_ref, bf16[1024,5504]{1,0:T(8,128)(2,1)} %w_hbm.1, f32[512,5504]{1,0:T(8,128)} %t_hbm.1), custom_call_target="tpu_custom_call" | custom-call | flops 17314086912 | bytes 112721920 | tf_op jit(solution)/shard_map/head/pallas_call | solution.py:408
  108.9 0.9 collective-permute-start
  109.9 1.6 collective-permute-start.1
  111.4 1.1 constant_dynamic-slice_fusion
  113.0 25.5 %collective-permute-done.2 = f32[128,1024]{1,0:T(8,128)S(1)} collective-permute-done((f32[128,1024]{1,0:T(8,128)S(1)}, f32[128,1024]{1,0:T(8,128)S(1)}, u32[]{:S(2)}, u32[]{:S(2)}) %collective-permute-start.2) | collective-permute-done | bytes 524320 | tf_op jit(solution)/shard_map/ppermute | solution.py:486
  138.6 1.1 dynamic-slice_add_fusion.du_ref.rest_0_
  140.5 16.1 %pool_backward.4 = (bf16[49,512,1024]{2,1,0:T(8,128)(2,1)}, f32[8,128]{1,0:T(8,128)}) custom-call(s32[1]{0:T(128)} %bitcast.6.off_ref, bf16[49,512,1024]{2,1,0:T(8,128)(2,1)} %bitcast.12, f32[128,1024]{1,0:T(8,128)} %copy-done.1, f32[1,1024]{1,0:T(1,128)} %bitcast.18, f32[128,1024]{1,0:T(8,128)} %copy-done.1), custom_call_target="tpu_custom_call" | custom-call | flops 3082813440 | bytes 25690112 | tf_op jit(solution)/shard_map/pool_backward/pallas_call | solution.py:99
  156.6 8.0 %collective-permute-done.3.du_ref = f32[128,1024]{1,0:T(8,128)S(1)} collective-permute-done((f32[128,1024]{1,0:T(8,128)S(1)}, f32[128,1024]{1,0:T(8,128)S(1)}, u32[]{:S(2)}, u32[]{:S(2)}) %collective-permute-start.3) | collective-permute-done | bytes 524320 | tf_op jit(solution)/shard_map/ppermute | solution.py:488
  165.4 16.1 %pool_backward.5 = (bf16[49,512,1024]{2,1,0:T(8,128)(2,1)}, f32[8,128]{1,0:T(8,128)}) custom-call(s32[1]{0:T(128)} %bitcast.5.off_ref, bf16[49,512,1024]{2,1,0:T(8,128)(2,1)} %bitcast.13, f32[128,1024]{1,0:T(8,128)} %copy-done.3, f32[1,1024]{1,0:T(1,128)} %bitcast.19, f32[8,128]{1,0:T(8,128)} %get-tuple-element.21.rest_0_, ...), custom_call_target="tpu_custom_call", output_to_operand_aliasing={{0}: (5, {})} | custom-call | flops 3082813440 | bytes 25690112 | tf_op jit(solution)/shard_map/pool_backward/pallas_call | solution.py:99
  181.4 1.3 slice.10
  182.7 4.5 %add_add_fusion.v_ref.rest_0_ = f32[128,5504]{1,0:T(8,128)S(1)} fusion(f32[128,5504]{1,0:T(8,128)} %collective-permute-done.1, f32[128,5504]{1,0:T(8,128)} %get-tuple-element.17, f32[128,5504]{1,0:T(8,128)} %collective-permute-done, f32[]{:T(128)} %bitcast.7), kind=kLoop, calls=%fused_computation | loop fusion | flops 2113536 | bytes 11272196 | tf_op jit(solution)/shard_map/add | solution.py:494
  187.8 62.7 %collective-permute-done.5 = f32[128,5504]{1,0:T(8,128)} collective-permute-done((f32[128,5504]{1,0:T(8,128)S(1)}, f32[128,5504]{1,0:T(8,128)}, u32[]{:S(2)}, u32[]{:S(2)}) %collective-permute-start.5) | collective-permute-done | bytes 2818080 | tf_op jit(solution)/shard_map/ppermute | solution.py:481
  254.0 4.1 %place_first.1 = f32[1024,5504]{1,0:T(8,128)} custom-call(s32[1]{0:T(128)} %bitcast.4.off_ref, f32[128,5504]{1,0:T(8,128)} %copy-done), custom_call_target="tpu_custom_call" | custom-call | flops 7045120 | bytes 5636096 | tf_op jit(solution)/shard_map/place_first/pallas_call | solution.py:131
  258.1 16.1 %pool_backward.6 = (bf16[49,512,1024]{2,1,0:T(8,128)(2,1)}, f32[8,128]{1,0:T(8,128)}) custom-call(s32[1]{0:T(128)} %bitcast.9.off_ref, bf16[49,512,1024]{2,1,0:T(8,128)(2,1)} %bitcast.14, f32[128,1024]{1,0:T(8,128)} %copy-done.5, f32[1,1024]{1,0:T(1,128)} %bitcast.20, f32[128,5504]{1,0:T(8,128)} %copy-done, ...), custom_call_target="tpu_custom_call", output_to_operand_aliasing={{0}: (5, {})} | custom-call | flops 3082813440 | bytes 25690112 | tf_op jit(solution)/shard_map/pool_backward/pallas_call | solution.py:99
  274.1 16.3 %pool_backward.7 = (bf16[49,512,1024]{2,1,0:T(8,128)(2,1)}, f32[8,128]{1,0:T(8,128)}) custom-call(s32[1]{0:T(128)} %bitcast.8.off_ref, bf16[49,512,1024]{2,1,0:T(8,128)(2,1)} %bitcast.15, f32[128,1024]{1,0:T(8,128)} %collective-permute-done.11.du_ref, f32[1,1024]{1,0:T(1,128)} %bitcast.21, ...), custom_call_target="tpu_custom_call", output_to_operand_aliasing={{0}: (5, {})} | custom-call | flops 3082813440 | bytes 25690112 | tf_op jit(solution)/shard_map/pool_backward/pallas_call | solution.py:99
  291.0 3.5 %constant_dynamic-update-slice_fusion.6 = f32[1024,5504]{1,0:T(8,128)} fusion(f32[1024,5504]{1,0:T(8,128)} %place_first.1, f32[128,5504]{1,0:T(8,128)} %collective-permute-done.4, s32[]{:T(128)S(6)} %select_n.38), kind=kLoop, calls=%fused_computation.9 | loop fusion | bytes 5636100 | tf_op jit(solution)/shard_map/dynamic_update_slice | solution.py:506
  294.5 3.5 %constant_dynamic-update-slice_fusion.5 = f32[1024,5504]{1,0:T(8,128)} fusion(f32[1024,5504]{1,0:T(8,128)} %constant_dynamic-update-slice_fusion.6, f32[128,5504]{1,0:T(8,128)} %collective-permute-done.5, s32[]{:T(128)S(6)} %select_n.39), kind=kLoop, calls=%fused_computation.8 | loop fusion | bytes 5636100 | tf_op jit(solution)/shard_map/dynamic_update_slice | solution.py:506
  298.1 3.5 %constant_dynamic-update-slice_fusion.4 = f32[1024,5504]{1,0:T(8,128)} fusion(f32[1024,5504]{1,0:T(8,128)} %constant_dynamic-update-slice_fusion.5, f32[128,5504]{1,0:T(8,128)} %collective-permute-done.6, s32[]{:T(128)S(6)} %select_n.40), kind=kLoop, calls=%fused_computation.7 | loop fusion | bytes 5636100 | tf_op jit(solution)/shard_map/dynamic_update_slice | solution.py:506
  301.6 3.5 %constant_dynamic-update-slice_fusion.3 = f32[1024,5504]{1,0:T(8,128)} fusion(f32[1024,5504]{1,0:T(8,128)} %constant_dynamic-update-slice_fusion.4, f32[128,5504]{1,0:T(8,128)} %collective-permute-done.7, s32[]{:T(128)S(6)} %select_n.41), kind=kLoop, calls=%fused_computation.6 | loop fusion | bytes 5636100 | tf_op jit(solution)/shard_map/dynamic_update_slice | solution.py:506
  305.1 1.7 constant_dynamic-update-slice_fusion.2
  306.9 3.5 %constant_dynamic-update-slice_fusion.1 = f32[1024,5504]{1,0:T(8,128)} fusion(f32[1024,5504]{1,0:T(8,128)} %constant_dynamic-update-slice_fusion.2, f32[128,5504]{1,0:T(8,128)} %collective-permute-done.9, s32[]{:T(128)S(6)} %select_n.43), kind=kLoop, calls=%fused_computation.4 | loop fusion | bytes 5636100 | tf_op jit(solution)/shard_map/dynamic_update_slice | solution.py:506
  310.4 1.7 constant_dynamic-update-slice_fusion
  (37 shorter events, 6.0 us)
Async XLA Ops:
  108.9 73.8 %collective-permute-start = (f32[128,5504]{1,0:T(8,128)}, f32[128,5504]{1,0:T(8,128)}, u32[]{:S(2)}, u32[]{:S(2)}) collective-permute-start(f32[128,5504]{1,0:T(8,128)} %get-tuple-element.18), channel_id=1, source_target_pairs={{0,2},{1,5},{2,0},{3,7},{4,6},{5,1},{6,4},{7,3},{8,10},{9,13},{10,... | collective-permute-start | bytes 8454152 | tf_op jit(solution)/shard_map/ppermute | solution.py:481
  109.9 72.9 %collective-permute-start.1 = (f32[128,5504]{1,0:T(8,128)}, f32[128,5504]{1,0:T(8,128)}, u32[]{:S(2)}, u32[]{:S(2)}) collective-permute-start(f32[128,5504]{1,0:T(8,128)} %get-tuple-element.19), channel_id=1, source_target_pairs={{0,4},{1,3},{2,6},{3,1},{4,0},{5,7},{6,2},{7,5},{8,12},{9,11},{10,... | collective-permute-start | bytes 8454152 | tf_op jit(solution)/shard_map/ppermute | solution.py:481
  112.5 26.0 %collective-permute-start.2 = (f32[128,1024]{1,0:T(8,128)S(1)}, f32[128,1024]{1,0:T(8,128)S(1)}, u32[]{:S(2)}, u32[]{:S(2)}) collective-permute-start(f32[128,1024]{1,0:T(8,128)S(1)} %constant_dynamic-slice_fusion), channel_id=1, source_target_pairs={{0,16},{8,24},{16,0},{24,8},{1,17},{9,25},{17,1},{25,9},{2,18},{10... | collective-permute-start | bytes 1572872 | tf_op jit(solution)/shard_map/ppermute | solution.py:486
  139.7 0.8 copy-start.1
  139.7 24.9 %collective-permute-start.3 = (f32[128,1024]{1,0:T(8,128)S(1)}, f32[128,1024]{1,0:T(8,128)S(1)}, u32[]{:S(2)}, u32[]{:S(2)}) collective-permute-start(f32[128,1024]{1,0:T(8,128)S(1)} %dynamic-slice_add_fusion.du_ref.rest_0_), channel_id=1, source_target_pairs={{0,16},{8,24},{16,0},{24,8},{1,17},{9,25},{17,1},{25,9},{2,18},{10... | collective-permute-start | bytes 1572872 | tf_op jit(solution)/shard_map/ppermute | solution.py:488
  164.6 0.8 copy-start.3
  181.4 6.3 %copy-start.2 = (f32[128,1024]{1,0:T(8,128)S(1)}, f32[128,1024]{1,0:T(8,128)}, u32[]{:S(2)}) copy-start(f32[128,1024]{1,0:T(8,128)} %copy-done.1) | copy-start | bytes 1572868
  181.4 70.7 %copy-start.4 = (f32[128,1024]{1,0:T(8,128)S(1)}, f32[128,1024]{1,0:T(8,128)}, u32[]{:S(2)}) copy-start(f32[128,1024]{1,0:T(8,128)} %copy-done.3) | copy-start | bytes 1572868
  181.4 70.7 %copy-start.6 = (f32[1,5632]{1,0:T(1,128)S(1)}, f32[1,5632]{1,0:T(1,128)}, u32[]{:S(2)}) copy-start(f32[1,5632]{1,0:T(1,128)} %get-tuple-element.16) | copy-start | bytes 67588
  187.3 66.7 %copy-start = (f32[128,5504]{1,0:T(8,128)}, f32[128,5504]{1,0:T(8,128)S(1)}, u32[]{:S(2)}) copy-start(f32[128,5504]{1,0:T(8,128)S(1)} %add_add_fusion.v_ref.rest_0_) | copy-start | bytes 8454148
  187.3 63.3 %collective-permute-start.5 = (f32[128,5504]{1,0:T(8,128)S(1)}, f32[128,5504]{1,0:T(8,128)}, u32[]{:S(2)}, u32[]{:S(2)}) collective-permute-start(f32[128,5504]{1,0:T(8,128)S(1)} %add_add_fusion.v_ref.rest_0_), channel_id=1, source_target_pairs={{0,4},{1,3},{2,6},{3,1},{4,0},{5,7},{6,2},{7,5},{8,12},{9,11},{10,... | collective-permute-start | bytes 8454152 | tf_op jit(solution)/shard_map/ppermute | solution.py:481
  187.4 103.1 %collective-permute-start.7 = (f32[128,5504]{1,0:T(8,128)S(1)}, f32[128,5504]{1,0:T(8,128)}, u32[]{:S(2)}, u32[]{:S(2)}) collective-permute-start(f32[128,5504]{1,0:T(8,128)S(1)} %add_add_fusion.v_ref.rest_0_), channel_id=1, source_target_pairs={{0,2},{1,5},{2,0},{3,7},{4,6},{5,1},{6,4},{7,3},{8,10},{9,13},{10,... | collective-permute-start | bytes 8454152 | tf_op jit(solution)/shard_map/ppermute | solution.py:481
  187.8 103.2 %collective-permute-start.4 = (f32[128,5504]{1,0:T(8,128)S(1)}, f32[128,5504]{1,0:T(8,128)}, u32[]{:S(2)}, u32[]{:S(2)}) collective-permute-start(f32[128,5504]{1,0:T(8,128)S(1)} %add_add_fusion.v_ref.rest_0_), channel_id=1, source_target_pairs={{0,1},{1,0},{2,3},{3,2},{4,5},{5,4},{6,7},{7,6},{8,9},{9,8},{10,11... | collective-permute-start | bytes 8454152 | tf_op jit(solution)/shard_map/ppermute | solution.py:481
  187.8 63.6 %collective-permute-start.12 = (f32[128,1024]{1,0:T(8,128)S(1)}, f32[128,1024]{1,0:T(8,128)S(1)}, u32[]{:S(2)}, u32[]{:S(2)}) collective-permute-start(f32[128,1024]{1,0:T(8,128)S(1)} %copy-done.2), channel_id=1, source_target_pairs={{0,8},{8,0},{16,24},{24,16},{1,9},{9,1},{17,25},{25,17},{2,10},{10... | collective-permute-start | bytes 1572872 | tf_op jit(solution)/shard_map/ppermute | solution.py:489
  250.5 47.5 %collective-permute-start.9 = (f32[128,5504]{1,0:T(8,128)}, f32[128,5504]{1,0:T(8,128)}, u32[]{:S(2)}, u32[]{:S(2)}) collective-permute-start(f32[128,5504]{1,0:T(8,128)} %collective-permute-done.5), channel_id=1, source_target_pairs={{0,2},{1,5},{2,0},{3,7},{4,6},{5,1},{6,4},{7,3},{8,10},{9,13},{10,... | collective-permute-start | bytes 8454152 | tf_op jit(solution)/shard_map/ppermute | solution.py:481
  251.3 46.7 %collective-permute-start.6 = (f32[128,5504]{1,0:T(8,128)}, f32[128,5504]{1,0:T(8,128)}, u32[]{:S(2)}, u32[]{:S(2)}) collective-permute-start(f32[128,5504]{1,0:T(8,128)} %collective-permute-done.5), channel_id=1, source_target_pairs={{0,1},{1,0},{2,3},{3,2},{4,5},{5,4},{6,7},{7,6},{8,9},{9,8},{10,11... | collective-permute-start | bytes 8454152 | tf_op jit(solution)/shard_map/ppermute | solution.py:481
  251.3 0.8 copy-start.5
  252.2 22.0 %collective-permute-start.11 = (f32[128,1024]{1,0:T(8,128)S(1)}, f32[128,1024]{1,0:T(8,128)}, u32[]{:S(2)}, u32[]{:S(2)}) collective-permute-start(f32[128,1024]{1,0:T(8,128)S(1)} %copy-done.4), channel_id=1, source_target_pairs={{0,8},{8,0},{16,24},{24,16},{1,9},{9,1},{17,25},{25,17},{2,10},{10... | collective-permute-start | bytes 1572872 | tf_op jit(solution)/shard_map/ppermute | solution.py:490
  290.4 14.7 %collective-permute-start.8 = (f32[128,5504]{1,0:T(8,128)}, f32[128,5504]{1,0:T(8,128)S(1)}, u32[]{:S(2)}, u32[]{:S(2)}) collective-permute-start(f32[128,5504]{1,0:T(8,128)} %collective-permute-done.7), channel_id=1, source_target_pairs={{0,1},{1,0},{2,3},{3,2},{4,5},{5,4},{6,7},{7,6},{8,9},{9,8},{10,11... | collective-permute-start | bytes 8454152 | tf_op jit(solution)/shard_map/ppermute | solution.py:481
  298.0 12.4 %collective-permute-start.10 = (f32[128,5504]{1,0:T(8,128)}, f32[128,5504]{1,0:T(8,128)S(1)}, u32[]{:S(2)}, u32[]{:S(2)}) collective-permute-start(f32[128,5504]{1,0:T(8,128)} %collective-permute-done.9), channel_id=1, source_target_pairs={{0,1},{1,0},{2,3},{3,2},{4,5},{5,4},{6,7},{7,6},{8,9},{9,8},{10,11... | collective-permute-start | bytes 8454152 | tf_op jit(solution)/shard_map/ppermute | solution.py:481

commit v2 on v1

--- a/solution.py
+++ b/solution.py
@@ -490,11 +490,11 @@
         du_last = lax.ppermute(du_far, "vp", near)
 
         dh, token = pool_backward(ht, du_own, gamma, None, 2 * z0 + z1, du_own)
-        dh, token = pool_backward(ht, du_far, gamma, dh, 2 * z0 + 1 - z1, token)
         d = ((d + r_d) + r_d2) + token[0, 0]
         c_fin = send(d, second)
         b_fin = send(d, first)
-        dh, token = pool_backward(ht, du_near, gamma, dh, 2 * (1 - z0) + z1, d)
+        dh, token = pool_backward(ht, du_far, gamma, dh, 2 * z0 + 1 - z1, d)
+        dh, token = pool_backward(ht, du_near, gamma, dh, 2 * (1 - z0) + z1, token)
         dh, token = pool_backward(ht, du_last, gamma, dh, 2 * (1 - z0) + 1 - z1, token)
         a_fin = send(c_fin, first)
         mine = [a_fin, b_fin, c_fin, d]
@@ -504,7 +504,8 @@
         for v, k in ((theirs[3], sib[3]), (mine[2], own[2]), (theirs[2], sib[2]),
                      (mine[1], own[1]), (theirs[1], sib[1]), (mine[0], own[0]), (theirs[0], sib[0])):
             out = lax.dynamic_update_slice(out, v, (k * part, 0))
-        return db[0, classes] / n_glob, out, db[0, :classes], dh.transpose(1, 0, 2)
+        loss, db = db[0, classes] / n_glob, db[0, :classes]
+        return loss, out, db, dh.transpose(1, 0, 2)
 
     return jax.shard_map(
         local_step,

time: 314 us -> 323 us (1.029)
  starting transfers between devices: 5 us -> 9.37 us
    ppermute x9, waiting for transfers between devices: 62.8 us -> 73.3 us  [send(): return lax.ppermute(v, 'dp', pairs)]
    ppermute x1, waiting for transfers between devices: 7.99 us -> 0.01 us  [local_step(): du_far = lax.ppermute(du_own, 'vp', distant)]
  transfers between devices with their start and end apart: 13 -> 13, of which waited for: 3 -> 4; matrix products, arithmetic and copies ran while one was open for 8% -> 8% of each run, Pallas kernels for 22% -> 21%
where the time goes in v2:
time: 323 us; the launch traced here: 322 us
  Pallas kernels  175 us (54%)
  waiting for transfers between devices  99 us (31%)
  local copies, waits for them, and re-layouts  29.7 us (9%)
  starting transfers between devices  9.37 us (3%)
  other arithmetic  6.45 us (2%)
    ppermute x9, waiting for transfers between devices, send(): return lax.ppermute(v, 'dp', pairs)  73.3 us
    pallas_call x1, Pallas kernels, head(): pl.pallas_call(functools.partial(head_kernel, n_glob), in_specs=[vmem, vm...  71.8 us
    pallas_call x4, Pallas kernels, pool_backward(): pl.pallas_call(pool_backward_kernel, grid_spec=pltpu.PrefetchScalarGridSp...  64.3 us
    pallas_call x1, Pallas kernels, pool_forward(): pl.pallas_call(pool_kernel, grid=(images // rows,), in_specs=[pl.BlockSpe...  35.1 us
    ppermute x1, waiting for transfers between devices, local_step(): lax.ppermute(lax.dynamic_slice(du_half, ((1 - z1) * quarter, 0), (quarter...  25.7 us
    dynamic_update_slice x7, local copies, waits for them, and re-layouts, local_step(): out = lax.dynamic_update_slice(out, v, (k * part, 0))  21.1 us
  transfers between devices with their start and end apart: 13, of which 4 were waited for; matrix products, arithmetic and copies ran while one was open for 8% of the time, Pallas kernels for 21%

profile of v2, /device:TPU:0, one launch (start us, length us, event | category | flops | bytes accessed | tf_op | source)
XLA Modules:
  0.0 322.3 jit_solution(4856356824393036171)
XLA Ops:
  0.6 1.4 broadcast_in_dim.30.b_ref
  2.0 35.1 %pool_forward.1.u_ref = bf16[512,1024]{1,0:T(8,128)(2,1)} custom-call(bf16[49,512,1024]{2,1,0:T(8,128)(2,1)} %bitcast.11, f32[1,1024]{1,0:T(1,128)} %bitcast.17, f32[1,1024]{1,0:T(1,128)} %bitcast.22), custom_call_target="tpu_custom_call" | custom-call | flops 8220835840 | bytes 51380224 | tf_op jit(solution)/shard_map/pool_forward/pallas_call | solution.py:44
  37.1 71.8 %head.1 = (f32[128,5504]{1,0:T(8,128)}, f32[128,5504]{1,0:T(8,128)}, f32[128,5504]{1,0:T(8,128)}, f32[256,1024]{1,0:T(8,128)}, f32[1,5632]{1,0:T(1,128)}) custom-call(bf16[512,1024]{1,0:T(8,128)(2,1)} %pool_forward.1.u_ref, f32[1,5504]{1,0:T(1,128)} %broadcast_in_dim.30.b_ref, bf16[1024,5504]{1,0:T(8,128)(2,1)} %w_hbm.1, f32[512,5504]{1,0:T(8,128)} %t_hbm.1), custom_call_target="tpu_custom_call" | custom-call | flops 17314086912 | bytes 112721920 | tf_op jit(solution)/shard_map/head/pallas_call | solution.py:408
  109.9 1.6 collective-permute-start.1
  111.4 1.9 constant_dynamic-slice_fusion
  113.8 25.7 %collective-permute-done.2 = f32[128,1024]{1,0:T(8,128)S(1)} collective-permute-done((f32[128,1024]{1,0:T(8,128)}, f32[128,1024]{1,0:T(8,128)S(1)}, u32[]{:S(2)}, u32[]{:S(2)}) %collective-permute-start.2) | collective-permute-done | bytes 524320 | tf_op jit(solution)/shard_map/ppermute | solution.py:486
  139.5 1.9 dynamic-slice_add_fusion.du_ref.rest_0_
  141.4 16.1 %pool_backward.4 = (bf16[49,512,1024]{2,1,0:T(8,128)(2,1)}, f32[8,128]{1,0:T(8,128)}) custom-call(s32[1]{0:T(128)} %bitcast.5.off_ref, bf16[49,512,1024]{2,1,0:T(8,128)(2,1)} %bitcast.12, f32[128,1024]{1,0:T(8,128)} %dynamic-slice_add_fusion.du_ref.rest_0_, f32[1,1024]{1,0:T(1,128)} %bitcast.18, f32[128,1024]{1,0:T(8,128)} %dynamic-slice_add_fusion.du_ref.rest_0_), custom_call_target="tpu_custom_call" | custom-call | flops 3082813440 | bytes 25690112 | tf_op jit(solution)/shard_map/pool_backward/pallas_call | solution.py:99
  158.8 13.8 %collective-permute-done = f32[128,5504]{1,0:T(8,128)S(1)} collective-permute-done((f32[128,5504]{1,0:T(8,128)}, f32[128,5504]{1,0:T(8,128)S(1)}, u32[]{:S(2)}, u32[]{:S(2)}) %collective-permute-start) | collective-permute-done | bytes 2818080 | tf_op jit(solution)/shard_map/ppermute | solution.py:481
  174.2 4.5 %add_add_fusion.v_ref.rest_0_ = f32[128,5504]{1,0:T(8,128)S(1)} fusion(f32[128,5504]{1,0:T(8,128)} %collective-permute-done.1, f32[128,5504]{1,0:T(8,128)} %get-tuple-element.17, f32[128,5504]{1,0:T(8,128)} %copy-done.2, f32[]{:T(128)} %bitcast.6), kind=kLoop, calls=%fused_computation | loop fusion | flops 2113536 | bytes 11272196 | tf_op jit(solution)/shard_map/add | solution.py:493
  178.7 2.0 collective-permute-start.4
  181.7 2.0 collective-permute-start.12
  183.7 59.1 %collective-permute-done.4 = f32[128,5504]{1,0:T(8,128)} collective-permute-done((f32[128,5504]{1,0:T(8,128)S(1)}, f32[128,5504]{1,0:T(8,128)}, u32[]{:S(2)}, u32[]{:S(2)}) %collective-permute-start.4) | collective-permute-done | bytes 2818080 | tf_op jit(solution)/shard_map/ppermute | solution.py:481
  245.6 4.1 %place_first.1 = f32[1024,5504]{1,0:T(8,128)} custom-call(s32[1]{0:T(128)} %bitcast.4.off_ref, f32[128,5504]{1,0:T(8,128)} %copy-done), custom_call_target="tpu_custom_call" | custom-call | flops 7045120 | bytes 5636096 | tf_op jit(solution)/shard_map/place_first/pallas_call | solution.py:131
  250.4 16.1 %pool_backward.5 = (bf16[49,512,1024]{2,1,0:T(8,128)(2,1)}, f32[8,128]{1,0:T(8,128)}) custom-call(s32[1]{0:T(128)} %bitcast.9.off_ref, bf16[49,512,1024]{2,1,0:T(8,128)(2,1)} %bitcast.13, f32[128,1024]{1,0:T(8,128)} %copy-done.3, f32[1,1024]{1,0:T(1,128)} %bitcast.19, f32[128,5504]{1,0:T(8,128)} %copy-done, ...), custom_call_target="tpu_custom_call", output_to_operand_aliasing={{0}: (5, {})} | custom-call | flops 3082813440 | bytes 25690112 | tf_op jit(solution)/shard_map/pool_backward/pallas_call | solution.py:99
  266.5 16.1 %pool_backward.6 = (bf16[49,512,1024]{2,1,0:T(8,128)(2,1)}, f32[8,128]{1,0:T(8,128)}) custom-call(s32[1]{0:T(128)} %bitcast.8.off_ref, bf16[49,512,1024]{2,1,0:T(8,128)(2,1)} %bitcast.14, f32[128,1024]{1,0:T(8,128)} %collective-permute-done.12.du_ref, f32[1,1024]{1,0:T(1,128)} %bitcast.20, ...), custom_call_target="tpu_custom_call", output_to_operand_aliasing={{0}: (5, {})} | custom-call | flops 3082813440 | bytes 25690112 | tf_op jit(solution)/shard_map/pool_backward/pallas_call | solution.py:99
  283.4 16.1 %pool_backward.7 = (bf16[49,512,1024]{2,1,0:T(8,128)(2,1)}, f32[8,128]{1,0:T(8,128)}) custom-call(s32[1]{0:T(128)} %bitcast.7.off_ref, bf16[49,512,1024]{2,1,0:T(8,128)(2,1)} %bitcast.15, f32[128,1024]{1,0:T(8,128)} %copy-done.4, f32[1,1024]{1,0:T(1,128)} %bitcast.21, f32[8,128]{1,0:T(8,128)} %get-tuple-element.25.rest_0_, ...), custom_call_target="tpu_custom_call", output_to_operand_aliasing={{0}: (5, {})} | custom-call | flops 3082813440 | bytes 25690112 | tf_op jit(solution)/shard_map/pool_backward/pallas_call | solution.py:99
  299.7 3.5 %constant_dynamic-update-slice_fusion.6 = f32[1024,5504]{1,0:T(8,128)} fusion(f32[1024,5504]{1,0:T(8,128)} %place_first.1, f32[128,5504]{1,0:T(8,128)} %collective-permute-done.3, s32[]{:T(128)S(6)} %select_n.38), kind=kLoop, calls=%fused_computation.9 | loop fusion | bytes 5636100 | tf_op jit(solution)/shard_map/dynamic_update_slice | solution.py:506
  303.3 3.5 %constant_dynamic-update-slice_fusion.5 = f32[1024,5504]{1,0:T(8,128)} fusion(f32[1024,5504]{1,0:T(8,128)} %constant_dynamic-update-slice_fusion.6, f32[128,5504]{1,0:T(8,128)} %collective-permute-done.4, s32[]{:T(128)S(6)} %select_n.39), kind=kLoop, calls=%fused_computation.8 | loop fusion | bytes 5636100 | tf_op jit(solution)/shard_map/dynamic_update_slice | solution.py:506
  307.1 3.5 %constant_dynamic-update-slice_fusion.4 = f32[1024,5504]{1,0:T(8,128)} fusion(f32[1024,5504]{1,0:T(8,128)} %constant_dynamic-update-slice_fusion.5, f32[128,5504]{1,0:T(8,128)} %collective-permute-done.5, s32[]{:T(128)S(6)} %select_n.40), kind=kLoop, calls=%fused_computation.7 | loop fusion | bytes 5636100 | tf_op jit(solution)/shard_map/dynamic_update_slice | solution.py:506
  310.6 3.5 %constant_dynamic-update-slice_fusion.3 = f32[1024,5504]{1,0:T(8,128)} fusion(f32[1024,5504]{1,0:T(8,128)} %constant_dynamic-update-slice_fusion.4, f32[128,5504]{1,0:T(8,128)} %collective-permute-done.6, s32[]{:T(128)S(6)} %select_n.41), kind=kLoop, calls=%fused_computation.6 | loop fusion | bytes 5636100 | tf_op jit(solution)/shard_map/dynamic_update_slice | solution.py:506
  314.2 1.7 constant_dynamic-update-slice_fusion.2
  315.9 3.5 %constant_dynamic-update-slice_fusion.1 = f32[1024,5504]{1,0:T(8,128)} fusion(f32[1024,5504]{1,0:T(8,128)} %constant_dynamic-update-slice_fusion.2, f32[128,5504]{1,0:T(8,128)} %collective-permute-done.8, s32[]{:T(128)S(6)} %select_n.43), kind=kLoop, calls=%fused_computation.4 | loop fusion | bytes 5636100 | tf_op jit(solution)/shard_map/dynamic_update_slice | solution.py:506
  319.4 1.7 constant_dynamic-update-slice_fusion
  (35 shorter events, 9.4 us)
Async XLA Ops:
  108.9 63.7 %collective-permute-start = (f32[128,5504]{1,0:T(8,128)}, f32[128,5504]{1,0:T(8,128)S(1)}, u32[]{:S(2)}, u32[]{:S(2)}) collective-permute-start(f32[128,5504]{1,0:T(8,128)} %get-tuple-element.18), channel_id=1, source_target_pairs={{0,2},{1,5},{2,0},{3,7},{4,6},{5,1},{6,4},{7,3},{8,10},{9,13},{10,... | collective-permute-start | bytes 8454152 | tf_op jit(solution)/shard_map/ppermute | solution.py:481
  109.9 63.0 %collective-permute-start.1 = (f32[128,5504]{1,0:T(8,128)}, f32[128,5504]{1,0:T(8,128)}, u32[]{:S(2)}, u32[]{:S(2)}) collective-permute-start(f32[128,5504]{1,0:T(8,128)} %get-tuple-element.19), channel_id=1, source_target_pairs={{0,4},{1,3},{2,6},{3,1},{4,0},{5,7},{6,2},{7,5},{8,12},{9,11},{10,... | collective-permute-start | bytes 8454152 | tf_op jit(solution)/shard_map/ppermute | solution.py:481
  113.3 26.2 %collective-permute-start.2 = (f32[128,1024]{1,0:T(8,128)}, f32[128,1024]{1,0:T(8,128)S(1)}, u32[]{:S(2)}, u32[]{:S(2)}) collective-permute-start(f32[128,1024]{1,0:T(8,128)} %constant_dynamic-slice_fusion), channel_id=1, source_target_pairs={{0,16},{8,24},{16,0},{24,8},{1,17},{9,25},{17,1},{25,9},{2,18},{10... | collective-permute-start | bytes 1572872 | tf_op jit(solution)/shard_map/ppermute | solution.py:486
  157.5 23.8 %copy-start.1 = (f32[128,1024]{1,0:T(8,128)S(1)}, f32[128,1024]{1,0:T(8,128)}, u32[]{:S(2)}) copy-start(f32[128,1024]{1,0:T(8,128)} %dynamic-slice_add_fusion.du_ref.rest_0_) | copy-start | bytes 1572868
  157.5 86.2 %copy-start.5 = (f32[1,5632]{1,0:T(1,128)S(1)}, f32[1,5632]{1,0:T(1,128)}, u32[]{:S(2)}) copy-start(f32[1,5632]{1,0:T(1,128)} %get-tuple-element.16) | copy-start | bytes 67588
  172.6 1.6 copy-start.2
  178.7 66.9 %copy-start = (f32[128,5504]{1,0:T(8,128)}, f32[128,5504]{1,0:T(8,128)S(1)}, u32[]{:S(2)}) copy-start(f32[128,5504]{1,0:T(8,128)S(1)} %add_add_fusion.v_ref.rest_0_) | copy-start | bytes 8454148
  178.7 64.1 %collective-permute-start.4 = (f32[128,5504]{1,0:T(8,128)S(1)}, f32[128,5504]{1,0:T(8,128)}, u32[]{:S(2)}, u32[]{:S(2)}) collective-permute-start(f32[128,5504]{1,0:T(8,128)S(1)} %add_add_fusion.v_ref.rest_0_), channel_id=1, source_target_pairs={{0,4},{1,3},{2,6},{3,1},{4,0},{5,7},{6,2},{7,5},{8,12},{9,11},{10,... | collective-permute-start | bytes 8454152 | tf_op jit(solution)/shard_map/ppermute | solution.py:481
  180.7 118.8 %collective-permute-start.6 = (f32[128,5504]{1,0:T(8,128)S(1)}, f32[128,5504]{1,0:T(8,128)}, u32[]{:S(2)}, u32[]{:S(2)}) collective-permute-start(f32[128,5504]{1,0:T(8,128)S(1)} %add_add_fusion.v_ref.rest_0_), channel_id=1, source_target_pairs={{0,2},{1,5},{2,0},{3,7},{4,6},{5,1},{6,4},{7,3},{8,10},{9,13},{10,... | collective-permute-start | bytes 8454152 | tf_op jit(solution)/shard_map/ppermute | solution.py:481
  181.3 118.4 %collective-permute-start.3 = (f32[128,5504]{1,0:T(8,128)S(1)}, f32[128,5504]{1,0:T(8,128)}, u32[]{:S(2)}, u32[]{:S(2)}) collective-permute-start(f32[128,5504]{1,0:T(8,128)S(1)} %add_add_fusion.v_ref.rest_0_), channel_id=1, source_target_pairs={{0,1},{1,0},{2,3},{3,2},{4,5},{5,4},{6,7},{7,6},{8,9},{9,8},{10,11... | collective-permute-start | bytes 8454152 | tf_op jit(solution)/shard_map/ppermute | solution.py:481
  181.3 61.6 %collective-permute-start.10 = (f32[128,1024]{1,0:T(8,128)S(1)}, f32[128,1024]{1,0:T(8,128)S(1)}, u32[]{:S(2)}, u32[]{:S(2)}) collective-permute-start(f32[128,1024]{1,0:T(8,128)S(1)} %copy-done.1), channel_id=1, source_target_pairs={{0,16},{8,24},{16,0},{24,8},{1,17},{9,25},{17,1},{25,9},{2,18},{10... | collective-permute-start | bytes 1572872 | tf_op jit(solution)/shard_map/ppermute | solution.py:488
  181.7 68.0 %collective-permute-start.12 = (f32[128,1024]{1,0:T(8,128)S(1)}, f32[128,1024]{1,0:T(8,128)}, u32[]{:S(2)}, u32[]{:S(2)}) collective-permute-start(f32[128,1024]{1,0:T(8,128)S(1)} %copy-done.1), channel_id=1, source_target_pairs={{0,8},{8,0},{16,24},{24,16},{1,9},{9,1},{17,25},{25,17},{2,10},{10... | collective-permute-start | bytes 1572872 | tf_op jit(solution)/shard_map/ppermute | solution.py:489
  242.8 64.0 %collective-permute-start.8 = (f32[128,5504]{1,0:T(8,128)}, f32[128,5504]{1,0:T(8,128)}, u32[]{:S(2)}, u32[]{:S(2)}) collective-permute-start(f32[128,5504]{1,0:T(8,128)} %collective-permute-done.4), channel_id=1, source_target_pairs={{0,2},{1,5},{2,0},{3,7},{4,6},{5,1},{6,4},{7,3},{8,10},{9,13},{10,... | collective-permute-start | bytes 8454152 | tf_op jit(solution)/shard_map/ppermute | solution.py:481
  242.9 0.8 copy-start.3
  243.8 63.3 %collective-permute-start.5 = (f32[128,5504]{1,0:T(8,128)}, f32[128,5504]{1,0:T(8,128)}, u32[]{:S(2)}, u32[]{:S(2)}) collective-permute-start(f32[128,5504]{1,0:T(8,128)} %collective-permute-done.4), channel_id=1, source_target_pairs={{0,1},{1,0},{2,3},{3,2},{4,5},{5,4},{6,7},{7,6},{8,9},{9,8},{10,11... | collective-permute-start | bytes 8454152 | tf_op jit(solution)/shard_map/ppermute | solution.py:481
  249.7 32.9 %collective-permute-start.11 = (f32[128,1024]{1,0:T(8,128)}, f32[128,1024]{1,0:T(8,128)S(1)}, u32[]{:S(2)}, u32[]{:S(2)}) collective-permute-start(f32[128,1024]{1,0:T(8,128)} %copy-done.3), channel_id=1, source_target_pairs={{0,8},{8,0},{16,24},{24,16},{1,9},{9,1},{17,25},{25,17},{2,10},{10... | collective-permute-start | bytes 1572872 | tf_op jit(solution)/shard_map/ppermute | solution.py:490
  282.6 0.8 copy-start.4
  299.5 14.7 %collective-permute-start.7 = (f32[128,5504]{1,0:T(8,128)}, f32[128,5504]{1,0:T(8,128)S(1)}, u32[]{:S(2)}, u32[]{:S(2)}) collective-permute-start(f32[128,5504]{1,0:T(8,128)} %collective-permute-done.6), channel_id=1, source_target_pairs={{0,1},{1,0},{2,3},{3,2},{4,5},{5,4},{6,7},{7,6},{8,9},{9,8},{10,11... | collective-permute-start | bytes 8454152 | tf_op jit(solution)/shard_map/ppermute | solution.py:481
  306.8 12.6 %collective-permute-start.9 = (f32[128,5504]{1,0:T(8,128)}, f32[128,5504]{1,0:T(8,128)S(1)}, u32[]{:S(2)}, u32[]{:S(2)}) collective-permute-start(f32[128,5504]{1,0:T(8,128)} %collective-permute-done.8), channel_id=1, source_target_pairs={{0,1},{1,0},{2,3},{3,2},{4,5},{5,4},{6,7},{7,6},{8,9},{9,8},{10,11... | collective-permute-start | bytes 8454152 | tf_op jit(solution)/shard_map/ppermute | solution.py:481

commit v3 on v2

--- a/solution.py
+++ b/solution.py
@@ -20,42 +20,6 @@
     c = x - x.sum(axis=-1, keepdims=True) * (1.0 / width)
     var = (c * c).sum(axis=-1, keepdims=True) * (1.0 / width)
     return c, lax.rsqrt(var + LN_EPS)
-
-
-def pool_kernel(h_ref, gamma_ref, beta_ref, u_ref, acc_ref):
-    tokens, rows, _ = h_ref.shape
-    acc_ref[...] = jnp.zeros_like(acc_ref)
-
-    def group(i, carry):
-        here = pl.ds(pl.multiple_of(i * 16, 16), 16)
-        for t in range(tokens):
-            c, r = norm_rows(h_ref[t, here, :].astype(F32))
-            acc_ref[here, :] += c * r
-        return carry
-
-    lax.fori_loop(0, rows // 16, group, 0)
-    u = acc_ref[...] * (gamma_ref[...] * (1.0 / tokens)) + beta_ref[...]
-    u_ref[...] = u.astype(BF16)
-
-
-def pool_forward(ht, gamma, beta, rows=32):
-    tokens, images, width = ht.shape
-    rows = min(rows, images)
-    return pl.pallas_call(
-        pool_kernel,
-        grid=(images // rows,),
-        in_specs=[
-            pl.BlockSpec((tokens, rows, width), lambda i: (0, i, 0)),
-            pl.BlockSpec((1, width), lambda i: (0, 0)),
-            pl.BlockSpec((1, width), lambda i: (0, 0)),
-        ],
-        out_specs=pl.BlockSpec((rows, width), lambda i: (i, 0)),
-        out_shape=jax.ShapeDtypeStruct((images, width), BF16),
-        scratch_shapes=[pltpu.VMEM((rows, width), F32)],
-        compiler_params=pltpu.CompilerParams(dimension_semantics=("arbitrary",)),
-        cost_estimate=pl.CostEstimate(flops=8 * ht.size * 40, bytes_accessed=2 * ht.size, transcendentals=0),
-        name="pool_forward",
-    )(ht, gamma[None], beta[None])
 
 
 def pool_backward_kernel(off_ref, h_ref, du_ref, gamma_ref, *rest):
@@ -143,17 +107,16 @@
 
 
 def head_kernel(
-    n_glob, u_ref, b_ref, w_hbm, t_hbm,
+    n_glob, h_hbm, gamma_ref, beta_ref, b_ref, w_hbm, t_hbm,
     pb_hbm, pc_hbm, pd_hbm, du_ref, db_ref,
-    w_s, t_s, z_s, ra_s, b_s, db_s, g_s, ut_s, m_s, s_s, ts_s, tz_s, stat_s, col_s, du_s, du_in,
-    load_sem, stat_send, stat_recv, sib_send, sib_recv, far_sem, du_sem, db_send, db_recv, out_sem, ready_sem,
+    h_s, acc_s, u_s, u_out, u_in, w_s, t_s, z_s, ra_s, b_s, db_s, g_s, ut_s, m_s, s_s, ts_s, tz_s, stat_s, col_s, du_s, du_in,
+    h_sem, load_sem, u_sem, stat_send, stat_recv, sib_send, sib_recv, far_sem, du_sem, db_send, db_recv, out_sem, ready_sem,
 ):
-    images, width = u_ref.shape
+    tokens, images, width = h_hbm.shape
     classes = w_hbm.shape[1]
     padded = w_s.shape[1]
     chunk = 512
     n_chunks = padded // chunk
-    tail = classes - (n_chunks - 1) * chunk
     part = width // 8
     half = images // 2
 
@@ -174,17 +137,29 @@
     for who in [(o, dp) for o in others] + [(vp, sib), (vp, along_x), (vp, along_y)]:
         pl.semaphore_signal(barrier, inc=1, device_id=who, device_id_type=MESH)
 
-    def loads(i, n):
-        cols = pl.ds(pl.multiple_of(i * chunk, chunk), n)
-        return (
-            pltpu.make_async_copy(w_hbm.at[:, cols], w_s.at[:, cols], load_sem.at[0, i]),
-            pltpu.make_async_copy(t_hbm.at[:, cols], t_s.at[pl.ds(0, images), cols], load_sem.at[1, i]),
-        )
-
-    ahead = min(4, n_chunks - 1)
-    for i in range(ahead):
-        for c in loads(i, chunk):
-            c.start()
+    quarter = images // 4
+    block = h_s.shape[2]
+    shared, blocks = quarter // block, 3 * quarter // block
+    n_loads = 1
+    while 2 * n_loads <= min(8, blocks):
+        n_loads *= 2
+
+    def first_row(i):
+        return pl.multiple_of(jnp.where(i < shared, z0 * quarter + i * block, half + (i - shared) * block), block)
+
+    def h_copy(i):
+        slot = lax.rem(i, 2)
+        return pltpu.make_async_copy(h_hbm.at[:, pl.ds(first_row(i), block), :], h_s.at[slot], h_sem.at[slot])
+
+    def load(i):
+        rows_w, rows_t = width // n_loads, images // n_loads
+        at_w = pl.ds(pl.multiple_of(i * rows_w, rows_w), rows_w)
+        at_t = pl.ds(pl.multiple_of(i * rows_t, rows_t), rows_t)
+        cols = pl.ds(0, classes)
+        pltpu.make_async_copy(w_hbm.at[at_w], w_s.at[at_w, cols], load_sem.at[0]).start()
+        pltpu.make_async_copy(t_hbm.at[at_t], t_s.at[at_t, cols], load_sem.at[1]).start()
+
+    h_copy(0).start()
     if padded > classes:
         b_s[:, classes:] = jnp.zeros((1, padded - classes), F32)
         w_s[:, classes:] = jnp.zeros((width, padded - classes), BF16)
@@ -196,29 +171,53 @@
     tz_s[...] = jnp.zeros_like(tz_s)
     limit = jnp.minimum(classes, NUM_CLASSES - vp * classes)
 
+    def pool(i, carry):
+        h_copy(i).wait()
+
+        @pl.when(i + 1 < blocks)
+        def _():
+            h_copy(i + 1).start()
+
+        @pl.when(i < n_loads)
+        def _():
+            load(i)
+
+        slot = lax.rem(i, 2)
+        acc_s[...] = jnp.zeros_like(acc_s)
+
+        def group(j, carry):
+            here = pl.ds(pl.multiple_of(j * 16, 16), 16)
+            for t in range(tokens):
+                c, r = norm_rows(h_s[slot, t, here, :].astype(F32))
+                acc_s[here, :] += c * r
+            return carry
+
+        lax.fori_loop(0, block // 16, group, 0)
+        u = acc_s[...] * (gamma_ref[...] * (1.0 / tokens)) + beta_ref[...]
+        u_s[pl.ds(first_row(i), block), :] = u.astype(BF16)
+
+        @pl.when(i < shared)
+        def _():
+            u_out[pl.ds(pl.multiple_of(i * block, block), block), :] = u
+
+        return carry
+
+    lax.fori_loop(0, shared, pool, 0)
+    pl.semaphore_wait(barrier, vp_size + 2)
+    u_copy = pltpu.make_async_remote_copy(
+        src_ref=u_out, dst_ref=u_in, send_sem=u_sem.at[0], recv_sem=u_sem.at[1],
+        device_id=(near, dp), device_id_type=MESH,
+    )
+    u_copy.start()
+    lax.fori_loop(shared, blocks, pool, 0)
+    u_copy.wait()
+    u_s[pl.ds(pl.multiple_of((1 - z0) * quarter, quarter), quarter), :] = u_in[...].astype(BF16)
+    pltpu.make_async_copy(w_hbm, w_s.at[:, pl.ds(0, classes)], load_sem.at[0]).wait()
+    pltpu.make_async_copy(t_hbm, t_s.at[pl.ds(0, images), pl.ds(0, classes)], load_sem.at[1]).wait()
+
     def logits(i, carry):
-        @pl.when(i + ahead < n_chunks - 1)
-        def _():
-            for c in loads(i + ahead, chunk):
-                c.start()
-
-        @pl.when(i + ahead == n_chunks - 1)
-        def _():
-            for c in loads(n_chunks - 1, tail):
-                c.start()
-
-        @pl.when(i < n_chunks - 1)
-        def _():
-            for c in loads(i, chunk):
-                c.wait()
-
-        @pl.when(i == n_chunks - 1)
-        def _():
-            for c in loads(n_chunks - 1, tail):
-                c.wait()
-
         cols = pl.ds(pl.multiple_of(i * chunk, chunk), chunk)
-        z = jnp.dot(u_ref[...], w_s[:, cols], preferred_element_type=F32) + b_s[:, cols]
+        z = jnp.dot(u_s[...], w_s[:, cols], preferred_element_type=F32) + b_s[:, cols]
         valid = i * chunk + lax.broadcasted_iota(jnp.int32, (1, chunk), 1) < limit
         t = t_s[:images, cols]
         tz = t * jnp.where(valid, z, 0.0)
@@ -252,8 +251,6 @@
     lane = lax.broadcasted_iota(jnp.int32, m_s.shape, 1)
     packed = jnp.where(lane == 0, m, jnp.where(lane == 1, s, jnp.where(lane == 2, ts, tz)))
     stat_s[vp] = packed.T[:8]
-
-    pl.semaphore_wait(barrier, vp_size + 2)
     copies = []
     for k, o in enumerate(others):
         c = pltpu.make_async_remote_copy(
@@ -262,7 +259,7 @@
         )
         c.start()
         copies.append(c)
-    ut_s[...] = u_ref[...].T
+    ut_s[...] = u_s[...].T
     for c in copies:
         c.wait()
 
@@ -306,7 +303,10 @@
 
     db_copies[0].start()
 
-    def dots(src, n, dst, add):
+    mid = (n_chunks + 1) // 2
+    split = mid * chunk
+
+    def dots(src, n, dst, add, lo=0, hi=n_chunks):
         left = ut_s[pl.ds(pl.multiple_of(src * part, part), n), :]
 
         def body(i, carry):
@@ -319,38 +319,50 @@
                 z_s[at, cols] = v
             return carry
 
-        lax.fori_loop(0, n_chunks, body, 0)
-
-    def to_sibling(k, at):
+        lax.fori_loop(lo, hi, body, 0)
+
+    def to_sibling(k, at, n, lo=0, hi=classes):
         rows = pl.ds(pl.multiple_of(at * part, part), part)
+        cols = pl.ds(lo, hi - lo)
         return pltpu.make_async_remote_copy(
-            src_ref=z_s.at[rows, pl.ds(0, classes)], dst_ref=t_s.at[pl.ds(k * part, part), pl.ds(0, classes)],
-            send_sem=sib_send.at[k], recv_sem=sib_recv.at[k], device_id=(vp, sib), device_id_type=MESH,
+            src_ref=z_s.at[rows, cols], dst_ref=t_s.at[pl.ds(k * part, part), cols],
+            send_sem=sib_send.at[n], recv_sem=sib_recv.at[n], device_id=(vp, sib), device_id_type=MESH,
         )
 
-    dots(4 * (1 - core) + 2 * (1 - p2), 2 * part, 0, False)
-    sends = [to_sibling(0, 1 - p1), to_sibling(1, p1), to_sibling(2, 3 - p1), to_sibling(3, 2 + p1)]
+    def to_first(n, lo, hi):
+        cols = pl.ds(lo, hi - lo)
+        return pltpu.make_async_remote_copy(
+            src_ref=t_s.at[pl.ds(0, part), cols], dst_ref=ra_s.at[:, cols],
+            send_sem=far_sem.at[0, n], recv_sem=far_sem.at[1, n], device_id=(vp, first), device_id_type=MESH,
+        )
+
+    halves = ((0, mid, 0, split), (mid, n_chunks, split, classes))
+    pair = 4 * (1 - core) + 2 * (1 - p2)
+    sends = [to_sibling(0, 0, n, lo, hi) for n, (_, _, lo, hi) in enumerate(halves)]
+    sends += [to_sibling(1, 1, 2), to_sibling(2, 3 - p1, 3), to_sibling(3, 2 + p1, 4)]
+    dots(pair + 1 - p1, part, 0, False, *halves[0][:2])
     pl.semaphore_wait(ready_sem, 1)
     sends[0].start()
+    dots(pair + 1 - p1, part, 0, False, *halves[1][:2])
+    sends[1].start()
     db_next(0)
+    dots(pair + p1, part, part, False)
+    sends[2].start()
+    db_next(1)
+    own = [4 * core + 2 * a + b for a, b in ((1 - p1, 1 - p2), (1 - p1, p2), (p1, 1 - p2), (p1, p2))]
+    far = []
+    for n, (i0, i1, lo, hi) in enumerate(halves):
+        sends[n].wait_recv()
+        dots(own[0], part, 0, True, i0, i1)
+        c = to_first(n, lo, hi)
+        c.start()
+        far.append(c)
     dots(4 * (1 - core) + 2 * p2, 2 * part, 2 * part, False)
-    sends[1].start()
-    db_next(1)
-
-    own = [4 * core + 2 * a + b for a, b in ((1 - p1, 1 - p2), (1 - p1, p2), (p1, 1 - p2), (p1, p2))]
+    sends[3].start()
+    sends[4].start()
 
     def piece(k):
         return t_s.at[pl.ds(k * part, part), pl.ds(0, classes)]
-
-    sends[0].wait_recv()
-    sends[2].start()
-    sends[3].start()
-    dots(own[0], part, 0, True)
-    far = pltpu.make_async_remote_copy(
-        src_ref=piece(0), dst_ref=ra_s, send_sem=far_sem.at[0], recv_sem=far_sem.at[1],
-        device_id=(vp, first), device_id_type=MESH,
-    )
-    far.start()
 
     def du_dot(i, carry):
         cols = pl.ds(pl.multiple_of(i * chunk, chunk), chunk)
@@ -371,7 +383,7 @@
 
     outs = []
     for k, out in ((1, pb_hbm), (2, pc_hbm), (3, pd_hbm)):
-        sends[k].wait_recv()
+        sends[k + 1].wait_recv()
         dots(own[k], part, k * part, True)
         c = pltpu.make_async_copy(piece(k), out, out_sem.at[k - 1])
         if k != 2:
@@ -381,7 +393,8 @@
         c.wait_send()
     du_copy.wait()
     du_ref[...] = du_s[keep, :] + du_in[...]
-    far.wait()
+    for c in far:
+        c.wait()
 
     def add_far(i, carry):
         cols = pl.ds(pl.multiple_of(i * 128, 128), 128)
@@ -395,25 +408,32 @@
         c.wait()
 
 
-def head(u, b, w, t, n_glob, vp_size):
-    images, width = u.shape
+def head(ht, gamma, beta, b, w, t, n_glob, vp_size):
+    tokens, images, width = ht.shape
     classes = w.shape[1]
     padded = (classes // 512 + 1) * 512
     part = width // 8
     rows = max(images, 4 * part)
+    quarter = images // 4
+    block = min(32, quarter)
     any_spec = pl.BlockSpec(memory_space=pl.ANY)
     vmem = pl.BlockSpec(memory_space=pltpu.VMEM)
     dma = pltpu.SemaphoreType.DMA
     piece = jax.ShapeDtypeStruct((part, classes), F32)
     return pl.pallas_call(
         functools.partial(head_kernel, n_glob),
-        in_specs=[vmem, vmem, any_spec, any_spec],
+        in_specs=[any_spec, vmem, vmem, vmem, any_spec, any_spec],
         out_specs=[any_spec] * 3 + [vmem] * 2,
         out_shape=[piece] * 3 + [
             jax.ShapeDtypeStruct((images // 2, width), F32),
             jax.ShapeDtypeStruct((1, padded), F32),
         ],
         scratch_shapes=[
+            pltpu.VMEM((2, tokens, block, width), BF16),
+            pltpu.VMEM((block, width), F32),
+            pltpu.VMEM((images, width), BF16),
+            pltpu.VMEM((quarter, width), F32),
+            pltpu.VMEM((quarter, width), F32),
             pltpu.VMEM((width, padded), BF16),
             pltpu.VMEM((rows, padded), F32),
             pltpu.VMEM((rows, padded), F32),
@@ -427,12 +447,14 @@
             pltpu.VMEM((images, 128), F32),
             pltpu.VMEM((images, width), F32),
             pltpu.VMEM((images // 2, width), F32),
-            dma((2, padded // 512)),
+            dma((2,)),
+            dma((2,)),
+            dma((2,)),
             dma((vp_size - 1,)),
             dma((vp_size - 1,)),
-            dma((4,)),
-            dma((4,)),
-            dma((2,)),
+            dma((5,)),
+            dma((5,)),
+            dma((2, 2)),
             dma((2,)),
             dma((3,)),
             dma((3,)),
@@ -446,7 +468,7 @@
             flops=6 * images * width * classes, bytes_accessed=20 * width * classes, transcendentals=0
         ),
         name="head",
-    )(u, b[None], w, t)
+    )(ht, gamma[None], beta[None], b[None], w, t)
 
 
 def solution(mesh):
@@ -474,8 +496,7 @@
         sib = [4 * (1 - core) + 2 * a + b for a, b in ((1 - p2, 1 - p1), (1 - p2, p1), (p2, 1 - p1), (p2, p1))]
 
         ht = h_loc.transpose(1, 0, 2)
-        u = pool_forward(ht, gamma, beta)
-        b, c, d, du_half, db = head(u, b_loc, w_loc, t_loc, n_glob, vp_size)
+        b, c, d, du_half, db = head(ht, gamma, beta, b_loc, w_loc, t_loc, n_glob, vp_size)
 
         def send(v, pairs):
             return lax.ppermute(v, "dp", pairs)

time: 323 us -> 316 us (0.978)
  Pallas kernels: 175 us -> 168 us
    pallas_call x2 -> x1, Pallas kernels: 107 us -> 99.5 us  [head(): pl.pallas_call(functools.partial(head_kernel, n_glob), in_specs=[any_spec...]
  transfers between devices with their start and end apart: 13 -> 13, of which waited for: 4 -> 3; matrix products, arithmetic and copies ran while one was open for 8% -> 8% of each run, Pallas kernels for 21% -> 22%
where the time goes in v3:
time: 316 us; the launch traced here: 315 us
  Pallas kernels  168 us (53%)
  waiting for transfers between devices  98.4 us (31%)
  local copies, waits for them, and re-layouts  30 us (9%)
  starting transfers between devices  10.1 us (3%)
  other arithmetic  6.45 us (2%)
    pallas_call x1, Pallas kernels, head(): pl.pallas_call(functools.partial(head_kernel, n_glob), in_specs=[any_spec...  99.5 us
    ppermute x9, waiting for transfers between devices, send(): return lax.ppermute(v, 'dp', pairs)  74 us
    pallas_call x4, Pallas kernels, pool_backward(): pl.pallas_call(pool_backward_kernel, grid_spec=pltpu.PrefetchScalarGridSp...  64.5 us
    ppermute x1, waiting for transfers between devices, local_step(): lax.ppermute(lax.dynamic_slice(du_half, ((1 - z1) * quarter, 0), (quarter...  24.3 us
    dynamic_update_slice x7, local copies, waits for them, and re-layouts, local_step(): out = lax.dynamic_update_slice(out, v, (k * part, 0))  21.1 us
  transfers between devices with their start and end apart: 13, of which 3 were waited for; matrix products, arithmetic and copies ran while one was open for 8% of the time, Pallas kernels for 22%

profile of v3, /device:TPU:0, one launch (start us, length us, event | category | flops | bytes accessed | tf_op | source)
XLA Modules:
  0.0 315.4 jit_solution(1755186662984810454)
XLA Ops:
  2.0 99.5 %head.1 = (f32[128,5504]{1,0:T(8,128)}, f32[128,5504]{1,0:T(8,128)}, f32[128,5504]{1,0:T(8,128)}, f32[256,1024]{1,0:T(8,128)}, f32[1,5632]{1,0:T(1,128)}) custom-call(bf16[49,512,1024]{2,1,0:T(8,128)(2,1)} %bitcast.11, f32[1,1024]{1,0:T(1,128)} %bitcast.17, f32[1,1024]{1,0:T(1,128)} %bitcast.22, f32[1,5504]{1,0:T(1,128)} %broadcast_in_dim.30.b_ref, ...), custom_call_target="tpu_custom_call" | custom-call | flops 17314086912 | bytes 112721920 | tf_op jit(solution)/shard_map/head/pallas_call | solution.py:423
  101.5 1.6 collective-permute-start
  103.0 1.5 collective-permute-start.1
  104.5 1.9 constant_dynamic-slice_fusion
  107.1 24.3 %collective-permute-done.2 = f32[128,1024]{1,0:T(8,128)S(1)} collective-permute-done((f32[128,1024]{1,0:T(8,128)}, f32[128,1024]{1,0:T(8,128)S(1)}, u32[]{:S(2)}, u32[]{:S(2)}) %collective-permute-start.2) | collective-permute-done | bytes 524320 | tf_op jit(solution)/shard_map/ppermute | solution.py:507
  131.4 1.9 dynamic-slice_add_fusion.du_ref.rest_0_
  133.3 16.1 %pool_backward.4 = (bf16[49,512,1024]{2,1,0:T(8,128)(2,1)}, f32[8,128]{1,0:T(8,128)}) custom-call(s32[1]{0:T(128)} %bitcast.5.off_ref, bf16[49,512,1024]{2,1,0:T(8,128)(2,1)} %bitcast.12, f32[128,1024]{1,0:T(8,128)} %dynamic-slice_add_fusion.du_ref.rest_0_, f32[1,1024]{1,0:T(1,128)} %bitcast.18, f32[128,1024]{1,0:T(8,128)} %dynamic-slice_add_fusion.du_ref.rest_0_), custom_call_target="tpu_custom_call" | custom-call | flops 3082813440 | bytes 25690112 | tf_op jit(solution)/shard_map/pool_backward/pallas_call | solution.py:63
  150.7 14.4 %collective-permute-done = f32[128,5504]{1,0:T(8,128)S(1)} collective-permute-done((f32[128,5504]{1,0:T(8,128)}, f32[128,5504]{1,0:T(8,128)S(1)}, u32[]{:S(2)}, u32[]{:S(2)}) %collective-permute-start) | collective-permute-done | bytes 2818080 | tf_op jit(solution)/shard_map/ppermute | solution.py:502
  165.1 1.6 copy-done.2
  166.7 4.5 %add_add_fusion.v_ref.rest_0_ = f32[128,5504]{1,0:T(8,128)S(1)} fusion(f32[128,5504]{1,0:T(8,128)} %collective-permute-done.1, f32[128,5504]{1,0:T(8,128)} %get-tuple-element.17, f32[128,5504]{1,0:T(8,128)} %copy-done.2, f32[]{:T(128)} %bitcast.6), kind=kLoop, calls=%fused_computation | loop fusion | flops 2113536 | bytes 11272196 | tf_op jit(solution)/shard_map/add | solution.py:514
  171.8 1.7 collective-permute-start.6
  174.2 1.5 collective-permute-start.12
  175.7 59.6 %collective-permute-done.4 = f32[128,5504]{1,0:T(8,128)} collective-permute-done((f32[128,5504]{1,0:T(8,128)S(1)}, f32[128,5504]{1,0:T(8,128)}, u32[]{:S(2)}, u32[]{:S(2)}) %collective-permute-start.4) | collective-permute-done | bytes 2818080 | tf_op jit(solution)/shard_map/ppermute | solution.py:502
  238.0 4.1 %place_first.1 = f32[1024,5504]{1,0:T(8,128)} custom-call(s32[1]{0:T(128)} %bitcast.4.off_ref, f32[128,5504]{1,0:T(8,128)} %copy-done), custom_call_target="tpu_custom_call" | custom-call | flops 7045120 | bytes 5636096 | tf_op jit(solution)/shard_map/place_first/pallas_call | solution.py:95
  243.3 16.1 %pool_backward.5 = (bf16[49,512,1024]{2,1,0:T(8,128)(2,1)}, f32[8,128]{1,0:T(8,128)}) custom-call(s32[1]{0:T(128)} %bitcast.9.off_ref, bf16[49,512,1024]{2,1,0:T(8,128)(2,1)} %bitcast.13, f32[128,1024]{1,0:T(8,128)} %copy-done.3, f32[1,1024]{1,0:T(1,128)} %bitcast.19, f32[128,5504]{1,0:T(8,128)} %copy-done, ...), custom_call_target="tpu_custom_call", output_to_operand_aliasing={{0}: (5, {})} | custom-call | flops 3082813440 | bytes 25690112 | tf_op jit(solution)/shard_map/pool_backward/pallas_call | solution.py:63
  259.4 16.3 %pool_backward.6 = (bf16[49,512,1024]{2,1,0:T(8,128)(2,1)}, f32[8,128]{1,0:T(8,128)}) custom-call(s32[1]{0:T(128)} %bitcast.8.off_ref, bf16[49,512,1024]{2,1,0:T(8,128)(2,1)} %bitcast.14, f32[128,1024]{1,0:T(8,128)} %collective-permute-done.12.du_ref, f32[1,1024]{1,0:T(1,128)} %bitcast.20, ...), custom_call_target="tpu_custom_call", output_to_operand_aliasing={{0}: (5, {})} | custom-call | flops 3082813440 | bytes 25690112 | tf_op jit(solution)/shard_map/pool_backward/pallas_call | solution.py:63
  276.5 16.1 %pool_backward.7 = (bf16[49,512,1024]{2,1,0:T(8,128)(2,1)}, f32[8,128]{1,0:T(8,128)}) custom-call(s32[1]{0:T(128)} %bitcast.7.off_ref, bf16[49,512,1024]{2,1,0:T(8,128)(2,1)} %bitcast.15, f32[128,1024]{1,0:T(8,128)} %copy-done.4, f32[1,1024]{1,0:T(1,128)} %bitcast.21, f32[8,128]{1,0:T(8,128)} %get-tuple-element.25.rest_0_, ...), custom_call_target="tpu_custom_call", output_to_operand_aliasing={{0}: (5, {})} | custom-call | flops 3082813440 | bytes 25690112 | tf_op jit(solution)/shard_map/pool_backward/pallas_call | solution.py:63
  292.8 3.5 %constant_dynamic-update-slice_fusion.6 = f32[1024,5504]{1,0:T(8,128)} fusion(f32[1024,5504]{1,0:T(8,128)} %place_first.1, f32[128,5504]{1,0:T(8,128)} %collective-permute-done.3, s32[]{:T(128)S(6)} %select_n.38), kind=kLoop, calls=%fused_computation.9 | loop fusion | bytes 5636100 | tf_op jit(solution)/shard_map/dynamic_update_slice | solution.py:527
  296.4 3.5 %constant_dynamic-update-slice_fusion.5 = f32[1024,5504]{1,0:T(8,128)} fusion(f32[1024,5504]{1,0:T(8,128)} %constant_dynamic-update-slice_fusion.6, f32[128,5504]{1,0:T(8,128)} %collective-permute-done.4, s32[]{:T(128)S(6)} %select_n.39), kind=kLoop, calls=%fused_computation.8 | loop fusion | bytes 5636100 | tf_op jit(solution)/shard_map/dynamic_update_slice | solution.py:527
  300.2 3.5 %constant_dynamic-update-slice_fusion.4 = f32[1024,5504]{1,0:T(8,128)} fusion(f32[1024,5504]{1,0:T(8,128)} %constant_dynamic-update-slice_fusion.5, f32[128,5504]{1,0:T(8,128)} %collective-permute-done.5, s32[]{:T(128)S(6)} %select_n.40), kind=kLoop, calls=%fused_computation.7 | loop fusion | bytes 5636100 | tf_op jit(solution)/shard_map/dynamic_update_slice | solution.py:527
  303.7 3.5 %constant_dynamic-update-slice_fusion.3 = f32[1024,5504]{1,0:T(8,128)} fusion(f32[1024,5504]{1,0:T(8,128)} %constant_dynamic-update-slice_fusion.4, f32[128,5504]{1,0:T(8,128)} %collective-permute-done.6, s32[]{:T(128)S(6)} %select_n.41), kind=kLoop, calls=%fused_computation.6 | loop fusion | bytes 5636100 | tf_op jit(solution)/shard_map/dynamic_update_slice | solution.py:527
  307.3 1.7 constant_dynamic-update-slice_fusion.2
  309.0 3.5 %constant_dynamic-update-slice_fusion.1 = f32[1024,5504]{1,0:T(8,128)} fusion(f32[1024,5504]{1,0:T(8,128)} %constant_dynamic-update-slice_fusion.2, f32[128,5504]{1,0:T(8,128)} %collective-permute-done.8, s32[]{:T(128)S(6)} %select_n.43), kind=kLoop, calls=%fused_computation.4 | loop fusion | bytes 5636100 | tf_op jit(solution)/shard_map/dynamic_update_slice | solution.py:527
  312.5 1.7 constant_dynamic-update-slice_fusion
  (34 shorter events, 9.2 us)
Async XLA Ops:
  101.5 63.6 %collective-permute-start = (f32[128,5504]{1,0:T(8,128)}, f32[128,5504]{1,0:T(8,128)S(1)}, u32[]{:S(2)}, u32[]{:S(2)}) collective-permute-start(f32[128,5504]{1,0:T(8,128)} %get-tuple-element.18), channel_id=1, source_target_pairs={{0,2},{1,5},{2,0},{3,7},{4,6},{5,1},{6,4},{7,3},{8,10},{9,13},{10,... | collective-permute-start | bytes 8454152 | tf_op jit(solution)/shard_map/ppermute | solution.py:502
  103.0 62.1 %collective-permute-start.1 = (f32[128,5504]{1,0:T(8,128)}, f32[128,5504]{1,0:T(8,128)}, u32[]{:S(2)}, u32[]{:S(2)}) collective-permute-start(f32[128,5504]{1,0:T(8,128)} %get-tuple-element.19), channel_id=1, source_target_pairs={{0,4},{1,3},{2,6},{3,1},{4,0},{5,7},{6,2},{7,5},{8,12},{9,11},{10,... | collective-permute-start | bytes 8454152 | tf_op jit(solution)/shard_map/ppermute | solution.py:502
  106.4 25.0 %collective-permute-start.2 = (f32[128,1024]{1,0:T(8,128)}, f32[128,1024]{1,0:T(8,128)S(1)}, u32[]{:S(2)}, u32[]{:S(2)}) collective-permute-start(f32[128,1024]{1,0:T(8,128)} %constant_dynamic-slice_fusion), channel_id=1, source_target_pairs={{0,16},{8,24},{16,0},{24,8},{1,17},{9,25},{17,1},{25,9},{2,18},{10... | collective-permute-start | bytes 1572872 | tf_op jit(solution)/shard_map/ppermute | solution.py:507
  149.4 24.1 %copy-start.1 = (f32[128,1024]{1,0:T(8,128)S(1)}, f32[128,1024]{1,0:T(8,128)}, u32[]{:S(2)}) copy-start(f32[128,1024]{1,0:T(8,128)} %dynamic-slice_add_fusion.du_ref.rest_0_) | copy-start | bytes 1572868
  149.4 86.7 %copy-start.5 = (f32[1,5632]{1,0:T(1,128)S(1)}, f32[1,5632]{1,0:T(1,128)}, u32[]{:S(2)}) copy-start(f32[1,5632]{1,0:T(1,128)} %get-tuple-element.16) | copy-start | bytes 67588
  165.1 1.6 copy-start.2
  171.2 66.8 %copy-start = (f32[128,5504]{1,0:T(8,128)}, f32[128,5504]{1,0:T(8,128)S(1)}, u32[]{:S(2)}) copy-start(f32[128,5504]{1,0:T(8,128)S(1)} %add_add_fusion.v_ref.rest_0_) | copy-start | bytes 8454148
  171.2 64.1 %collective-permute-start.4 = (f32[128,5504]{1,0:T(8,128)S(1)}, f32[128,5504]{1,0:T(8,128)}, u32[]{:S(2)}, u32[]{:S(2)}) collective-permute-start(f32[128,5504]{1,0:T(8,128)S(1)} %add_add_fusion.v_ref.rest_0_), channel_id=1, source_target_pairs={{0,4},{1,3},{2,6},{3,1},{4,0},{5,7},{6,2},{7,5},{8,12},{9,11},{10,... | collective-permute-start | bytes 8454152 | tf_op jit(solution)/shard_map/ppermute | solution.py:502
  171.8 120.8 %collective-permute-start.6 = (f32[128,5504]{1,0:T(8,128)S(1)}, f32[128,5504]{1,0:T(8,128)}, u32[]{:S(2)}, u32[]{:S(2)}) collective-permute-start(f32[128,5504]{1,0:T(8,128)S(1)} %add_add_fusion.v_ref.rest_0_), channel_id=1, source_target_pairs={{0,2},{1,5},{2,0},{3,7},{4,6},{5,1},{6,4},{7,3},{8,10},{9,13},{10,... | collective-permute-start | bytes 8454152 | tf_op jit(solution)/shard_map/ppermute | solution.py:502
  173.5 119.3 %collective-permute-start.3 = (f32[128,5504]{1,0:T(8,128)S(1)}, f32[128,5504]{1,0:T(8,128)}, u32[]{:S(2)}, u32[]{:S(2)}) collective-permute-start(f32[128,5504]{1,0:T(8,128)S(1)} %add_add_fusion.v_ref.rest_0_), channel_id=1, source_target_pairs={{0,1},{1,0},{2,3},{3,2},{4,5},{5,4},{6,7},{7,6},{8,9},{9,8},{10,11... | collective-permute-start | bytes 8454152 | tf_op jit(solution)/shard_map/ppermute | solution.py:502
  173.5 61.8 %collective-permute-start.10 = (f32[128,1024]{1,0:T(8,128)S(1)}, f32[128,1024]{1,0:T(8,128)S(1)}, u32[]{:S(2)}, u32[]{:S(2)}) collective-permute-start(f32[128,1024]{1,0:T(8,128)S(1)} %copy-done.1), channel_id=1, source_target_pairs={{0,16},{8,24},{16,0},{24,8},{1,17},{9,25},{17,1},{25,9},{2,18},{10... | collective-permute-start | bytes 1572872 | tf_op jit(solution)/shard_map/ppermute | solution.py:509
  174.2 67.8 %collective-permute-start.12 = (f32[128,1024]{1,0:T(8,128)S(1)}, f32[128,1024]{1,0:T(8,128)}, u32[]{:S(2)}, u32[]{:S(2)}) collective-permute-start(f32[128,1024]{1,0:T(8,128)S(1)} %copy-done.1), channel_id=1, source_target_pairs={{0,8},{8,0},{16,24},{24,16},{1,9},{9,1},{17,25},{25,17},{2,10},{10... | collective-permute-start | bytes 1572872 | tf_op jit(solution)/shard_map/ppermute | solution.py:510
  235.3 64.6 %collective-permute-start.8 = (f32[128,5504]{1,0:T(8,128)}, f32[128,5504]{1,0:T(8,128)}, u32[]{:S(2)}, u32[]{:S(2)}) collective-permute-start(f32[128,5504]{1,0:T(8,128)} %collective-permute-done.4), channel_id=1, source_target_pairs={{0,2},{1,5},{2,0},{3,7},{4,6},{5,1},{6,4},{7,3},{8,10},{9,13},{10,... | collective-permute-start | bytes 8454152 | tf_op jit(solution)/shard_map/ppermute | solution.py:502
  235.3 0.8 copy-start.3
  236.1 64.1 %collective-permute-start.5 = (f32[128,5504]{1,0:T(8,128)}, f32[128,5504]{1,0:T(8,128)}, u32[]{:S(2)}, u32[]{:S(2)}) collective-permute-start(f32[128,5504]{1,0:T(8,128)} %collective-permute-done.4), channel_id=1, source_target_pairs={{0,1},{1,0},{2,3},{3,2},{4,5},{5,4},{6,7},{7,6},{8,9},{9,8},{10,11... | collective-permute-start | bytes 8454152 | tf_op jit(solution)/shard_map/ppermute | solution.py:502
  242.0 33.7 %collective-permute-start.11 = (f32[128,1024]{1,0:T(8,128)}, f32[128,1024]{1,0:T(8,128)S(1)}, u32[]{:S(2)}, u32[]{:S(2)}) collective-permute-start(f32[128,1024]{1,0:T(8,128)} %copy-done.3), channel_id=1, source_target_pairs={{0,8},{8,0},{16,24},{24,16},{1,9},{9,1},{17,25},{25,17},{2,10},{10... | collective-permute-start | bytes 1572872 | tf_op jit(solution)/shard_map/ppermute | solution.py:511
  275.7 0.8 copy-start.4
  292.6 14.7 %collective-permute-start.7 = (f32[128,5504]{1,0:T(8,128)}, f32[128,5504]{1,0:T(8,128)S(1)}, u32[]{:S(2)}, u32[]{:S(2)}) collective-permute-start(f32[128,5504]{1,0:T(8,128)} %collective-permute-done.6), channel_id=1, source_target_pairs={{0,1},{1,0},{2,3},{3,2},{4,5},{5,4},{6,7},{7,6},{8,9},{9,8},{10,11... | collective-permute-start | bytes 8454152 | tf_op jit(solution)/shard_map/ppermute | solution.py:502
  299.9 12.6 %collective-permute-start.9 = (f32[128,5504]{1,0:T(8,128)}, f32[128,5504]{1,0:T(8,128)S(1)}, u32[]{:S(2)}, u32[]{:S(2)}) collective-permute-start(f32[128,5504]{1,0:T(8,128)} %collective-permute-done.8), channel_id=1, source_target_pairs={{0,1},{1,0},{2,3},{3,2},{4,5},{5,4},{6,7},{7,6},{8,9},{9,8},{10,11... | collective-permute-start | bytes 8454152 | tf_op jit(solution)/shard_map/ppermute | solution.py:502

commit v4 on v3

--- a/solution.py
+++ b/solution.py
@@ -310,7 +310,7 @@
         left = ut_s[pl.ds(pl.multiple_of(src * part, part), n), :]
 
         def body(i, carry):
-            cols = pl.ds(pl.multiple_of(i * chunk, chunk), chunk)
+            cols = pl.ds(i * chunk if isinstance(i, int) else pl.multiple_of(i * chunk, chunk), chunk)
             v = jnp.dot(left, g_s[:, cols], preferred_element_type=F32)
             at = pl.ds(dst, n)
             if add:
@@ -319,7 +319,11 @@
                 z_s[at, cols] = v
             return carry
 
-        lax.fori_loop(lo, hi, body, 0)
+        if n == part and hi - lo < n_chunks:
+            for i in range(lo, hi):
+                body(i, 0)
+        else:
+            lax.fori_loop(lo, hi, body, 0)
 
     def to_sibling(k, at, n, lo=0, hi=classes):
         rows = pl.ds(pl.multiple_of(at * part, part), part)
@@ -357,53 +361,60 @@
         c = to_first(n, lo, hi)
         c.start()
         far.append(c)
-    dots(4 * (1 - core) + 2 * p2, 2 * part, 2 * part, False)
-    sends[3].start()
-    sends[4].start()
 
     def piece(k):
         return t_s.at[pl.ds(k * part, part), pl.ds(0, classes)]
 
-    def du_dot(i, carry):
-        cols = pl.ds(pl.multiple_of(i * chunk, chunk), chunk)
-        v = lax.dot_general(g_s[:, cols], w_s[:, cols], (((1,), (1,)), ((), ())), preferred_element_type=F32)
-        du_s[...] = du_s[...] + v
-        return carry
+    def du_dots(at):
+        def body(i, carry):
+            cols = pl.ds(pl.multiple_of(i * chunk, chunk), chunk)
+            v = lax.dot_general(g_s[at, cols], w_s[:, cols], (((1,), (1,)), ((), ())), preferred_element_type=F32)
+            du_s[at, :] = du_s[at, :] + v
+            return carry
+
+        lax.fori_loop(0, n_chunks, body, 0)
 
     du_s[...] = jnp.zeros_like(du_s)
-    lax.fori_loop(0, n_chunks, du_dot, 0)
     keep = pl.ds(pl.multiple_of(z0 * half, half), half)
     give = pl.ds(pl.multiple_of((1 - z0) * half, half), half)
+    du_dots(give)
     du_copy = pltpu.make_async_remote_copy(
         src_ref=du_s.at[give], dst_ref=du_in, send_sem=du_sem.at[0], recv_sem=du_sem.at[1],
         device_id=(near, dp), device_id_type=MESH,
     )
     du_copy.start()
+    dots(4 * (1 - core) + 2 * p2, 2 * part, 2 * part, False)
+    sends[3].start()
+    sends[4].start()
     db_next(2)
+    du_dots(keep)
 
     outs = []
-    for k, out in ((1, pb_hbm), (2, pc_hbm), (3, pd_hbm)):
+    for k, out in ((1, pb_hbm), (2, None), (3, pd_hbm)):
         sends[k + 1].wait_recv()
         dots(own[k], part, k * part, True)
-        c = pltpu.make_async_copy(piece(k), out, out_sem.at[k - 1])
-        if k != 2:
+        if out is not None:
+            c = pltpu.make_async_copy(piece(k), out, out_sem.at[k - 1])
             c.start()
-        outs.append(c)
+            outs.append(c)
     for c in sends:
         c.wait_send()
     du_copy.wait()
     du_ref[...] = du_s[keep, :] + du_in[...]
-    for c in far:
-        c.wait()
-
-    def add_far(i, carry):
-        cols = pl.ds(pl.multiple_of(i * 128, 128), 128)
-        at = pl.ds(2 * part, part)
-        t_s[at, cols] = t_s[at, cols] + ra_s[:, cols]
-        return carry
-
-    lax.fori_loop(0, classes // 128, add_far, 0)
-    outs[1].start()
+    for n, (_, _, lo, hi) in enumerate(halves):
+        far[n].wait()
+
+        def add_far(i, carry):
+            cols = pl.ds(pl.multiple_of(i * 128, 128), 128)
+            at = pl.ds(2 * part, part)
+            t_s[at, cols] = t_s[at, cols] + ra_s[:, cols]
+            return carry
+
+        lax.fori_loop(lo // 128, hi // 128, add_far, 0)
+        cols = pl.ds(lo, hi - lo)
+        c = pltpu.make_async_copy(t_s.at[pl.ds(2 * part, part), cols], pc_hbm.at[:, cols], out_sem.at[1 + 2 * n])
+        c.start()
+        outs.append(c)
     for c in outs:
         c.wait()
 
@@ -458,7 +469,7 @@
             dma((2,)),
             dma((3,)),
             dma((3,)),
-            dma((3,)),
+            dma((4,)),
             pltpu.SemaphoreType.REGULAR,
         ],
         compiler_params=pltpu.CompilerParams(
@@ -517,14 +528,18 @@
         dh, token = pool_backward(ht, du_far, gamma, dh, 2 * z0 + 1 - z1, d)
         dh, token = pool_backward(ht, du_near, gamma, dh, 2 * (1 - z0) + z1, token)
         dh, token = pool_backward(ht, du_last, gamma, dh, 2 * (1 - z0) + 1 - z1, token)
-        a_fin = send(c_fin, first)
-        mine = [a_fin, b_fin, c_fin, d]
+        a_fin = []
+        for k in range(2):
+            a_fin.append(send(c_fin[k * part // 2 : (k + 1) * part // 2], first))
+        mine = a_fin + [b_fin, c_fin, d]
         theirs = [send(v, sibling) for v in mine]
 
         out = place_first(d, own[3], width)
-        for v, k in ((theirs[3], sib[3]), (mine[2], own[2]), (theirs[2], sib[2]),
-                     (mine[1], own[1]), (theirs[1], sib[1]), (mine[0], own[0]), (theirs[0], sib[0])):
-            out = lax.dynamic_update_slice(out, v, (k * part, 0))
+        places = [(theirs[4], sib[3], 0), (mine[3], own[2], 0), (theirs[3], sib[2], 0), (mine[2], own[1], 0),
+                  (theirs[2], sib[1], 0), (mine[0], own[0], 0), (theirs[0], sib[0], 0),
+                  (mine[1], own[0], part // 2), (theirs[1], sib[0], part // 2)]
+        for v, k, off in places:
+            out = lax.dynamic_update_slice(out, v, (k * part + off, 0))
         loss, db = db[0, classes] / n_glob, db[0, :classes]
         return loss, out, db, dh.transpose(1, 0, 2)
 

time: 316 us -> 292 us (0.924)
  waiting for transfers between devices: 98.4 us -> 82.7 us
  Pallas kernels: 168 us -> 161 us
    ppermute x9 -> x11, waiting for transfers between devices: 74 us -> 39.5 us  [send(): return lax.ppermute(v, 'dp', pairs)]
    ppermute x1, waiting for transfers between devices: 0.01 us -> 19.4 us  [local_step(): du_far = lax.ppermute(du_own, 'vp', distant)]
    pallas_call x1, Pallas kernels: 99.5 us -> 92.5 us  [head(): pl.pallas_call(functools.partial(head_kernel, n_glob), in_specs=[any_spec...]
    dynamic_update_slice x7 -> x9, local copies, waits for them, and re-layouts: 21.1 us -> 18.8 us  [local_step(): out = lax.dynamic_update_slice(out, v, (k * part + off, 0))]
    ppermute x9 -> x11, starting transfers between devices: 5.95 us -> 7.83 us  [send(): return lax.ppermute(v, 'dp', pairs)]
  transfers between devices with their start and end apart: 13 -> 15, of which waited for: 3 -> 5; matrix products, arithmetic and copies ran while one was open for 8% -> 9% of each run, Pallas kernels for 22% -> 24%
where the time goes in v4:
time: 292 us; the launch traced here: 291 us
  Pallas kernels  161 us (55%)
  waiting for transfers between devices  82.7 us (28%)
  local copies, waits for them, and re-layouts  27.9 us (10%)
  starting transfers between devices  10.2 us (3%)
  other arithmetic  6.5 us (2%)
    pallas_call x1, Pallas kernels, head(): pl.pallas_call(functools.partial(head_kernel, n_glob), in_specs=[any_spec...  92.5 us
    pallas_call x4, Pallas kernels, pool_backward(): pl.pallas_call(pool_backward_kernel, grid_spec=pltpu.PrefetchScalarGridSp...  64.5 us
    ppermute x11, waiting for transfers between devices, send(): return lax.ppermute(v, 'dp', pairs)  39.5 us
    ppermute x1, waiting for transfers between devices, local_step(): lax.ppermute(lax.dynamic_slice(du_half, ((1 - z1) * quarter, 0), (quarter...  23.9 us
    ppermute x1, waiting for transfers between devices, local_step(): du_far = lax.ppermute(du_own, 'vp', distant)  19.4 us
    dynamic_update_slice x9, local copies, waits for them, and re-layouts, local_step(): out = lax.dynamic_update_slice(out, v, (k * part + off, 0))  18.8 us
    ppermute x11, starting transfers between devices, send(): return lax.ppermute(v, 'dp', pairs)  7.83 us
  transfers between devices with their start and end apart: 15, of which 5 were waited for; matrix products, arithmetic and copies ran while one was open for 9% of the time, Pallas kernels for 24%

profile of v4, /device:TPU:0, one launch (start us, length us, event | category | flops | bytes accessed | tf_op | source)
XLA Modules:
  0.0 290.8 jit_solution(8534040928384541665)
XLA Ops:
  2.0 92.5 %head.1 = (f32[128,5504]{1,0:T(8,128)}, f32[128,5504]{1,0:T(8,128)}, f32[128,5504]{1,0:T(8,128)}, f32[256,1024]{1,0:T(8,128)}, f32[1,5632]{1,0:T(1,128)}) custom-call(bf16[49,512,1024]{2,1,0:T(8,128)(2,1)} %bitcast.11, f32[1,1024]{1,0:T(1,128)} %bitcast.17, f32[1,1024]{1,0:T(1,128)} %bitcast.22, f32[1,5504]{1,0:T(1,128)} %broadcast_in_dim.30.b_ref, ...), custom_call_target="tpu_custom_call" | custom-call | flops 17314086912 | bytes 112721920 | tf_op jit(solution)/shard_map/head/pallas_call | solution.py:434
  95.7 1.5 collective-permute-start.1
  97.2 1.9 constant_dynamic-slice_fusion
  100.1 23.9 %collective-permute-done.2 = f32[128,1024]{1,0:T(8,128)S(1)} collective-permute-done((f32[128,1024]{1,0:T(8,128)}, f32[128,1024]{1,0:T(8,128)S(1)}, u32[]{:S(2)}, u32[]{:S(2)}) %collective-permute-start.2) | collective-permute-done | bytes 524320 | tf_op jit(solution)/shard_map/ppermute | solution.py:518
  123.9 1.9 dynamic-slice_add_fusion.du_ref.rest_0_
  125.8 16.1 %pool_backward.4 = (bf16[49,512,1024]{2,1,0:T(8,128)(2,1)}, f32[8,128]{1,0:T(8,128)}) custom-call(s32[1]{0:T(128)} %bitcast.5.off_ref, bf16[49,512,1024]{2,1,0:T(8,128)(2,1)} %bitcast.12, f32[128,1024]{1,0:T(8,128)} %dynamic-slice_add_fusion.du_ref.rest_0_, f32[1,1024]{1,0:T(1,128)} %bitcast.18, f32[128,1024]{1,0:T(8,128)} %dynamic-slice_add_fusion.du_ref.rest_0_), custom_call_target="tpu_custom_call" | custom-call | flops 3082813440 | bytes 25690112 | tf_op jit(solution)/shard_map/pool_backward/pallas_call | solution.py:63
  143.1 14.8 %collective-permute-done = f32[128,5504]{1,0:T(8,128)S(1)} collective-permute-done((f32[128,5504]{1,0:T(8,128)}, f32[128,5504]{1,0:T(8,128)S(1)}, u32[]{:S(2)}, u32[]{:S(2)}) %collective-permute-start) | collective-permute-done | bytes 2818080 | tf_op jit(solution)/shard_map/ppermute | solution.py:513
  157.9 1.6 copy-done.2
  159.5 4.6 %add_add_fusion.v_ref.rest_0_ = f32[128,5504]{1,0:T(8,128)S(1)} fusion(f32[128,5504]{1,0:T(8,128)} %collective-permute-done.1, f32[128,5504]{1,0:T(8,128)} %get-tuple-element.17, f32[128,5504]{1,0:T(8,128)} %copy-done.2, f32[]{:T(128)} %bitcast.6), kind=kLoop, calls=%fused_computation | loop fusion | flops 2113536 | bytes 11272196 | tf_op jit(solution)/shard_map/add | solution.py:525
  164.1 1.6 collective-permute-start.4
  170.2 19.4 %collective-permute-done.12.du_ref = f32[128,1024]{1,0:T(8,128)} collective-permute-done((f32[128,1024]{1,0:T(8,128)S(1)}, f32[128,1024]{1,0:T(8,128)}, u32[]{:S(2)}, u32[]{:S(2)}) %collective-permute-start.12) | collective-permute-done | bytes 524320 | tf_op jit(solution)/shard_map/ppermute | solution.py:520
  189.6 4.1 %place_first.1 = f32[1024,5504]{1,0:T(8,128)} custom-call(s32[1]{0:T(128)} %bitcast.4.off_ref, f32[128,5504]{1,0:T(8,128)} %copy-done), custom_call_target="tpu_custom_call" | custom-call | flops 7045120 | bytes 5636096 | tf_op jit(solution)/shard_map/place_first/pallas_call | solution.py:95
  193.6 16.1 %pool_backward.5 = (bf16[49,512,1024]{2,1,0:T(8,128)(2,1)}, f32[8,128]{1,0:T(8,128)}) custom-call(s32[1]{0:T(128)} %bitcast.9.off_ref, bf16[49,512,1024]{2,1,0:T(8,128)(2,1)} %bitcast.13, f32[128,1024]{1,0:T(8,128)} %collective-permute-done.12.du_ref, f32[1,1024]{1,0:T(1,128)} %bitcast.19, f32[128,5504]{1,0:T(8,128)} %copy-done, ...), custom_call_target="tpu_custom_call", output_to_operand_aliasing={{0}: (5, {})} | custom-call | flops 3082813440 | bytes 25690112 | tf_op jit(solution)/shard_map/pool_backward/pallas_call | solution.py:63
  209.7 16.3 %pool_backward.6 = (bf16[49,512,1024]{2,1,0:T(8,128)(2,1)}, f32[8,128]{1,0:T(8,128)}) custom-call(s32[1]{0:T(128)} %bitcast.8.off_ref, bf16[49,512,1024]{2,1,0:T(8,128)(2,1)} %bitcast.14, f32[128,1024]{1,0:T(8,128)} %collective-permute-done.14.du_ref, f32[1,1024]{1,0:T(1,128)} %bitcast.20, ...), custom_call_target="tpu_custom_call", output_to_operand_aliasing={{0}: (5, {})} | custom-call | flops 3082813440 | bytes 25690112 | tf_op jit(solution)/shard_map/pool_backward/pallas_call | solution.py:63
  226.0 16.1 %pool_backward.7 = (bf16[49,512,1024]{2,1,0:T(8,128)(2,1)}, f32[8,128]{1,0:T(8,128)}) custom-call(s32[1]{0:T(128)} %bitcast.7.off_ref, bf16[49,512,1024]{2,1,0:T(8,128)(2,1)} %bitcast.15, f32[128,1024]{1,0:T(8,128)} %collective-permute-done.13.du_ref, f32[1,1024]{1,0:T(1,128)} %bitcast.21, ...), custom_call_target="tpu_custom_call", output_to_operand_aliasing={{0}: (5, {})} | custom-call | flops 3082813440 | bytes 25690112 | tf_op jit(solution)/shard_map/pool_backward/pallas_call | solution.py:63
  242.2 2.0 fusion
  244.6 1.6 collective-permute-start.10
  246.2 3.5 %constant_dynamic-update-slice_fusion.8 = f32[1024,5504]{1,0:T(8,128)} fusion(f32[1024,5504]{1,0:T(8,128)} %place_first.1, f32[128,5504]{1,0:T(8,128)} %collective-permute-done.3, s32[]{:T(128)S(6)} %select_n.44), kind=kLoop, calls=%fused_computation.11 | loop fusion | bytes 5636100 | tf_op jit(solution)/shard_map/dynamic_update_slice | solution.py:542
  249.8 3.5 %constant_dynamic-update-slice_fusion.7 = f32[1024,5504]{1,0:T(8,128)} fusion(f32[1024,5504]{1,0:T(8,128)} %constant_dynamic-update-slice_fusion.8, f32[128,5504]{1,0:T(8,128)} %collective-permute-done.4, s32[]{:T(128)S(6)} %select_n.45), kind=kLoop, calls=%fused_computation.10 | loop fusion | bytes 5636100 | tf_op jit(solution)/shard_map/dynamic_update_slice | solution.py:542
  253.3 9.5 %collective-permute-done.8 = f32[64,5504]{1,0:T(8,128)S(1)} collective-permute-done((f32[64,5504]{1,0:T(8,128)S(1)}, f32[64,5504]{1,0:T(8,128)S(1)}, u32[]{:S(2)}, u32[]{:S(2)}) %collective-permute-start.8) | collective-permute-done | bytes 1409056 | tf_op jit(solution)/shard_map/ppermute | solution.py:513
  262.9 15.1 %collective-permute-done.10 = f32[64,5504]{1,0:T(8,128)S(1)} collective-permute-done((f32[64,5504]{1,0:T(8,128)S(1)}, f32[64,5504]{1,0:T(8,128)S(1)}, u32[]{:S(2)}, u32[]{:S(2)}) %collective-permute-start.10) | collective-permute-done | bytes 1409056 | tf_op jit(solution)/shard_map/ppermute | solution.py:513
  278.0 1.7 constant_dynamic-update-slice_fusion.6
  279.7 3.5 %constant_dynamic-update-slice_fusion.5 = f32[1024,5504]{1,0:T(8,128)} fusion(f32[1024,5504]{1,0:T(8,128)} %constant_dynamic-update-slice_fusion.6, f32[128,5504]{1,0:T(8,128)} %collective-permute-done.6, s32[]{:T(128)S(6)} %select_n.47), kind=kLoop, calls=%fused_computation.8 | loop fusion | bytes 5636100 | tf_op jit(solution)/shard_map/dynamic_update_slice | solution.py:542
  283.2 1.7 constant_dynamic-update-slice_fusion.4
  (37 shorter events, 13.9 us)
Async XLA Ops:
  94.4 63.5 %collective-permute-start = (f32[128,5504]{1,0:T(8,128)}, f32[128,5504]{1,0:T(8,128)S(1)}, u32[]{:S(2)}, u32[]{:S(2)}) collective-permute-start(f32[128,5504]{1,0:T(8,128)} %get-tuple-element.18), channel_id=1, source_target_pairs={{0,2},{1,5},{2,0},{3,7},{4,6},{5,1},{6,4},{7,3},{8,10},{9,13},{10,... | collective-permute-start | bytes 8454152 | tf_op jit(solution)/shard_map/ppermute | solution.py:513
  95.7 62.2 %collective-permute-start.1 = (f32[128,5504]{1,0:T(8,128)}, f32[128,5504]{1,0:T(8,128)}, u32[]{:S(2)}, u32[]{:S(2)}) collective-permute-start(f32[128,5504]{1,0:T(8,128)} %get-tuple-element.19), channel_id=1, source_target_pairs={{0,4},{1,3},{2,6},{3,1},{4,0},{5,7},{6,2},{7,5},{8,12},{9,11},{10,... | collective-permute-start | bytes 8454152 | tf_op jit(solution)/shard_map/ppermute | solution.py:513
  99.1 24.8 %collective-permute-start.2 = (f32[128,1024]{1,0:T(8,128)}, f32[128,1024]{1,0:T(8,128)S(1)}, u32[]{:S(2)}, u32[]{:S(2)}) collective-permute-start(f32[128,1024]{1,0:T(8,128)} %constant_dynamic-slice_fusion), channel_id=1, source_target_pairs={{0,16},{8,24},{16,0},{24,8},{1,17},{9,25},{17,1},{25,9},{2,18},{10... | collective-permute-start | bytes 1572872 | tf_op jit(solution)/shard_map/ppermute | solution.py:518
  157.9 1.6 copy-start.2
  159.5 6.2 %copy-start.1 = (f32[128,1024]{1,0:T(8,128)S(1)}, f32[128,1024]{1,0:T(8,128)}, u32[]{:S(2)}) copy-start(f32[128,1024]{1,0:T(8,128)} %dynamic-slice_add_fusion.du_ref.rest_0_) | copy-start | bytes 1572868
  159.5 8.9 %copy-start.3 = (f32[1,5632]{1,0:T(1,128)S(1)}, f32[1,5632]{1,0:T(1,128)}, u32[]{:S(2)}) copy-start(f32[1,5632]{1,0:T(1,128)} %get-tuple-element.16) | copy-start | bytes 67588
  164.1 25.5 %copy-start = (f32[128,5504]{1,0:T(8,128)}, f32[128,5504]{1,0:T(8,128)S(1)}, u32[]{:S(2)}) copy-start(f32[128,5504]{1,0:T(8,128)S(1)} %add_add_fusion.v_ref.rest_0_) | copy-start | bytes 8454148
  164.1 78.0 %collective-permute-start.4 = (f32[128,5504]{1,0:T(8,128)S(1)}, f32[128,5504]{1,0:T(8,128)}, u32[]{:S(2)}, u32[]{:S(2)}) collective-permute-start(f32[128,5504]{1,0:T(8,128)S(1)} %add_add_fusion.v_ref.rest_0_), channel_id=1, source_target_pairs={{0,4},{1,3},{2,6},{3,1},{4,0},{5,7},{6,2},{7,5},{8,12},{9,11},{10,... | collective-permute-start | bytes 8454152 | tf_op jit(solution)/shard_map/ppermute | solution.py:513
  165.7 23.9 %collective-permute-start.12 = (f32[128,1024]{1,0:T(8,128)S(1)}, f32[128,1024]{1,0:T(8,128)}, u32[]{:S(2)}, u32[]{:S(2)}) collective-permute-start(f32[128,1024]{1,0:T(8,128)S(1)} %copy-done.1), channel_id=1, source_target_pairs={{0,16},{8,24},{16,0},{24,8},{1,17},{9,25},{17,1},{25,9},{2,18},{10... | collective-permute-start | bytes 1572872 | tf_op jit(solution)/shard_map/ppermute | solution.py:520
  166.6 79.7 %collective-permute-start.6 = (f32[128,5504]{1,0:T(8,128)S(1)}, f32[128,5504]{1,0:T(8,128)}, u32[]{:S(2)}, u32[]{:S(2)}) collective-permute-start(f32[128,5504]{1,0:T(8,128)S(1)} %add_add_fusion.v_ref.rest_0_), channel_id=1, source_target_pairs={{0,2},{1,5},{2,0},{3,7},{4,6},{5,1},{6,4},{7,3},{8,10},{9,13},{10,... | collective-permute-start | bytes 8454152 | tf_op jit(solution)/shard_map/ppermute | solution.py:513
  167.9 78.4 %collective-permute-start.3 = (f32[128,5504]{1,0:T(8,128)S(1)}, f32[128,5504]{1,0:T(8,128)}, u32[]{:S(2)}, u32[]{:S(2)}) collective-permute-start(f32[128,5504]{1,0:T(8,128)S(1)} %add_add_fusion.v_ref.rest_0_), channel_id=1, source_target_pairs={{0,1},{1,0},{2,3},{3,2},{4,5},{5,4},{6,7},{7,6},{8,9},{9,8},{10,11... | collective-permute-start | bytes 8454152 | tf_op jit(solution)/shard_map/ppermute | solution.py:513
  167.9 41.8 %collective-permute-start.14 = (f32[128,1024]{1,0:T(8,128)S(1)}, f32[128,1024]{1,0:T(8,128)}, u32[]{:S(2)}, u32[]{:S(2)}) collective-permute-start(f32[128,1024]{1,0:T(8,128)S(1)} %copy-done.1), channel_id=1, source_target_pairs={{0,8},{8,0},{16,24},{24,16},{1,9},{9,1},{17,25},{25,17},{2,10},{10... | collective-permute-start | bytes 1572872 | tf_op jit(solution)/shard_map/ppermute | solution.py:521
  189.6 36.4 %collective-permute-start.13 = (f32[128,1024]{1,0:T(8,128)}, f32[128,1024]{1,0:T(8,128)}, u32[]{:S(2)}, u32[]{:S(2)}) collective-permute-start(f32[128,1024]{1,0:T(8,128)} %collective-permute-done.12.du_ref), channel_id=1, source_target_pairs={{0,8},{8,0},{16,24},{24,16},{1,9},{9,1},{17,25},{25,17},{2,10},{10... | collective-permute-start | bytes 1572872 | tf_op jit(solution)/shard_map/ppermute | solution.py:522
  242.1 35.9 %collective-permute-start.5 = (f32[128,5504]{1,0:T(8,128)}, f32[128,5504]{1,0:T(8,128)S(1)}, u32[]{:S(2)}, u32[]{:S(2)}) collective-permute-start(f32[128,5504]{1,0:T(8,128)} %collective-permute-done.4), channel_id=1, source_target_pairs={{0,1},{1,0},{2,3},{3,2},{4,5},{5,4},{6,7},{7,6},{8,9},{9,8},{10,11... | collective-permute-start | bytes 8454152 | tf_op jit(solution)/shard_map/ppermute | solution.py:513
  244.1 18.7 %collective-permute-start.8 = (f32[64,5504]{1,0:T(8,128)S(1)}, f32[64,5504]{1,0:T(8,128)S(1)}, u32[]{:S(2)}, u32[]{:S(2)}) collective-permute-start(f32[64,5504]{1,0:T(8,128)S(1)} %get-tuple-element.29), channel_id=1, source_target_pairs={{0,2},{1,5},{2,0},{3,7},{4,6},{5,1},{6,4},{7,3},{8,10},{9,13},{10,... | collective-permute-start | bytes 4227080 | tf_op jit(solution)/shard_map/ppermute | solution.py:513
  244.6 33.4 %collective-permute-start.10 = (f32[64,5504]{1,0:T(8,128)S(1)}, f32[64,5504]{1,0:T(8,128)S(1)}, u32[]{:S(2)}, u32[]{:S(2)}) collective-permute-start(f32[64,5504]{1,0:T(8,128)S(1)} %get-tuple-element.28), channel_id=1, source_target_pairs={{0,2},{1,5},{2,0},{3,7},{4,6},{5,1},{6,4},{7,3},{8,10},{9,13},{10,... | collective-permute-start | bytes 4227080 | tf_op jit(solution)/shard_map/ppermute | solution.py:513
  246.2 37.0 %collective-permute-start.7 = (f32[128,5504]{1,0:T(8,128)}, f32[128,5504]{1,0:T(8,128)S(1)}, u32[]{:S(2)}, u32[]{:S(2)}) collective-permute-start(f32[128,5504]{1,0:T(8,128)} %collective-permute-done.6), channel_id=1, source_target_pairs={{0,1},{1,0},{2,3},{3,2},{4,5},{5,4},{6,7},{7,6},{8,9},{9,8},{10,11... | collective-permute-start | bytes 8454152 | tf_op jit(solution)/shard_map/ppermute | solution.py:513
  262.9 23.3 %collective-permute-start.9 = (f32[64,5504]{1,0:T(8,128)S(1)}, f32[64,5504]{1,0:T(8,128)S(1)}, u32[]{:S(2)}, u32[]{:S(2)}) collective-permute-start(f32[64,5504]{1,0:T(8,128)S(1)} %collective-permute-done.8), channel_id=1, source_target_pairs={{0,1},{1,0},{2,3},{3,2},{4,5},{5,4},{6,7},{7,6},{8,9},{9,8},{10,11... | collective-permute-start | bytes 4227080 | tf_op jit(solution)/shard_map/ppermute | solution.py:513
  278.0 10.6 %collective-permute-start.11 = (f32[64,5504]{1,0:T(8,128)S(1)}, f32[64,5504]{1,0:T(8,128)S(1)}, u32[]{:S(2)}, u32[]{:S(2)}) collective-permute-start(f32[64,5504]{1,0:T(8,128)S(1)} %collective-permute-done.10), channel_id=1, source_target_pairs={{0,1},{1,0},{2,3},{3,2},{4,5},{5,4},{6,7},{7,6},{8,9},{9,8},{10,11... | collective-permute-start | bytes 4227080 | tf_op jit(solution)/shard_map/ppermute | solution.py:513
